TPU v7x, 256 devices: a whole 4x4x8 slice. The times are simulated.
256 devices in a mesh: island: 4 (over z_lo), fsdp: 64 (over z_hi, x, y, core).
Axes of the slice: x: 4, y: 4, z: 8 (z_hi: 2, z_lo: 4; z = z_hi * 4 + z_lo), core: 2. Of those that a mesh axis runs over, the one named last changes fastest.
Arguments:
- grads: bfloat16 [4, 1, 14336, 4096], P('island', None, 'fsdp'), may hold values from -200 to 200
- buffer: bfloat16 [4, 14336, 4096], P('island', 'fsdp'), may hold values from -200 to 200
- q_old: float32 [4, 4096, 128], P('island', 'fsdp'), may hold values from -0.09375 to 0.09375
- anchor: bfloat16 [14336, 4096], P('fsdp'), may hold values from -6 to 6
- momentum: float32 [14336, 4096], P(('fsdp', 'island')), may hold values from -6 to 6
Outputs:
- anchor_new: bfloat16 [14336, 4096], P('fsdp')
- buffer_new: bfloat16 [4, 14336, 4096], P('island', 'fsdp')
- momentum_new: float32 [14336, 4096], P(('fsdp', 'island'))
All inputs are finite; a program needn't handle non-finite values.
Results may differ from a plain program's by a relative error of at most 0.012.
Values may be sent and summed in bfloat16 or wider, within the bound.
A program may use at most 64 MiB of HBM per device.

v0:
```python
import math

import jax
import jax.numpy as jnp
from jax import lax
from jax.sharding import Mesh
from jax.sharding import PartitionSpec as P

ROWS = 14336
COLS = 4096
RANK = 128
FSDP = ("fsdp_0", "fsdp_1", "fsdp_2", "fsdp_3")
FSDP_ISLAND = ("fsdp_0", "fsdp_1", "fsdp_2", "fsdp_3", "island")


precise = lax.Precision.HIGHEST
error_decay = 0.95
outer_beta = 0.9
outer_rate = 0.7
epsilon = 1e-06


def from_everyone(shard, axis):
    devices = lax.axis_size(axis)
    return lax.all_to_all(
        jnp.broadcast_to(shard[None], (devices, *shard.shape)), axis, 0, 0, tiled=True
    )


def laid_out(tiles, dim):
    dims = list(tiles.shape[1:])
    dims[dim] *= tiles.shape[0]
    return jnp.moveaxis(tiles, 0, dim).reshape(dims)


def whole_of(shard, axes, dim):
    far, near = axes
    initial = from_everyone(shard, far)
    tiles = jnp.swapaxes(from_everyone(initial, near), 0, 1)
    return laid_out(tiles.reshape(-1, *shard.shape), dim)


def rows_for(lines, devices):
    spare = -lines.shape[0] % devices
    if not spare:
        return lines
    return jnp.concatenate([lines, jnp.zeros((spare, *lines.shape[1:]), lines.dtype)])


def split_up(shard, dim, devices):
    before, after = (shard.shape[:dim], shard.shape[dim + 1 :])
    return jnp.moveaxis(shard.reshape(*before, devices, -1, *after), dim, 0)


def sent_and_summed(shard, axis, dim):
    devices = lax.axis_size(axis)
    tiles = lax.all_to_all(split_up(shard, dim, devices), axis, 0, 0, tiled=True)
    return jnp.sum(tiles.astype(jnp.float32), axis=0)


def sum_by_axis(shard, axes, dim):
    far, near = axes
    tiles = split_up(shard, dim, lax.axis_size(far))
    nearer = sent_and_summed(tiles, near, dim + 1)
    arrived = lax.all_to_all(
        nearer.astype(jnp.bfloat16), far, split_axis=0, concat_axis=0, tiled=True
    )
    return arrived.astype(jnp.float32).sum(axis=0)


def sum_by_parts(shard, axes):
    lines = shard.reshape(-1, shard.shape[-1])
    padded = rows_for(lines, lax.axis_size(axes[0]) * lax.axis_size(axes[1]))
    whole = whole_of(sum_by_axis(padded, axes, 0).astype(jnp.bfloat16), axes, 0)
    return lax.slice_in_dim(whole, 0, len(lines)).reshape(shard.shape).astype(jnp.float32)


def collect(shard, axis, dim):
    return laid_out(from_everyone(shard, axis), dim)


def product(left_side, right_side, left_dims, right_dims):
    return lax.dot_general(
        left_side,
        right_side,
        (((left_dims,), (right_dims,)), ((), ())),
        precision=precise,
        preferred_element_type=jnp.float32,
    )


def inverse_upper(lower_factor):
    identity = jnp.eye(lower_factor.shape[0], dtype=lower_factor.dtype)
    return lax.linalg.triangular_solve(
        lower_factor, identity, left_side=True, lower=True, transpose_a=True
    )


def body(grads, buffer, q_old, anchor, momentum):
    rate = math.sqrt(ROWS * COLS / RANK)
    matrix = buffer[0].astype(jnp.float32) + grads[0, 0].astype(jnp.float32)
    raw_image = product(
        matrix,
        whole_of(
            q_old[0].astype(jnp.bfloat16), (("fsdp_0", "fsdp_1", "fsdp_2"), "fsdp_3"), 0
        ).astype(jnp.float32),
        1,
        0,
    )
    q_basis = None
    projected = sum_by_parts(
        product(matrix, raw_image, 0, 0).astype(jnp.bfloat16),
        (("fsdp_0", "fsdp_1", "fsdp_2"), "fsdp_3"),
    )
    gram_matrix = sum_by_parts(
        product(raw_image, raw_image, 0, 0).astype(jnp.bfloat16),
        (("fsdp_0", "fsdp_1", "fsdp_2"), "fsdp_3"),
    )
    upper_inverse = inverse_upper(jnp.linalg.cholesky(gram_matrix))
    basis_rows = product(raw_image, upper_inverse, 1, 0)
    factor = product(projected, upper_inverse, 1, 0)
    q_basis = factor / jnp.sqrt(jnp.sum(factor * factor, axis=0) + epsilon)
    residue = matrix - (1.0 - error_decay) * product(basis_rows, factor, 1, 1)
    moved_sum = rate * product(basis_rows, q_basis, 1, 1)
    delta_total = sent_and_summed(moved_sum.astype(jnp.bfloat16), "island", 0)
    delta_mean = delta_total / lax.axis_size("island")
    momentum_new = outer_beta * momentum + delta_mean
    piece_rows = momentum.shape[0]
    anchor_piece = lax.dynamic_slice_in_dim(
        anchor, lax.axis_index("island") * piece_rows, piece_rows, 0
    ).astype(jnp.float32)
    anchor_share = (anchor_piece - outer_rate * (delta_mean + outer_beta * momentum_new)).astype(
        jnp.bfloat16
    )
    anchor_new = collect(anchor_share, "island", 0)
    return (anchor_new, residue[None].astype(jnp.bfloat16), momentum_new)


def solution(mesh):
    split = Mesh(
        mesh.devices.reshape(mesh.shape["island"], 2, 4, 4, 2),
        ("island", "fsdp_0", "fsdp_1", "fsdp_2", "fsdp_3"),
    )
    return jax.shard_map(
        body,
        mesh=split,
        in_specs=(
            P("island", None, FSDP, None),
            P("island", FSDP, None),
            P("island", FSDP, None),
            P(FSDP, None),
            P(FSDP_ISLAND, None),
        ),
        out_specs=(P(FSDP, None), P("island", FSDP, None), P(FSDP_ISLAND, None)),
        check_vma=False,
    )
```

profile of v0, /device:TPU:1, one launch (start us, length us, event | category | flops | bytes accessed | tf_op | source)
XLA Modules:
  0.0 259.1 jit_solution(5315260585218657379)
XLA Ops:
  0.6 0.8 convert_bitcast_fusion.5
  1.4 0.1 broadcast_in_dim.18
  1.5 28.0 %all_to_all.60 = bf16[32,64,128]{2,1,0:T(8,128)(2,1)S(1)} all-to-all(bf16[32,64,128]{2,1,0:T(8,128)(2,1)S(1)} %broadcast_in_dim.18), channel_id=1, replica_groups=mesh['island'=4,'fsdp_0'=2,'fsdp_1'=4,'fsdp_2'=4,'fsdp_3'=2] {'fsdp_0','..., dimensions={0} | all-to-all | bytes 1048576 | tf_op jit(solution)/shard_map/all_to_all | solution.py:25
  29.5 0.3 broadcast_in_dim.19
  29.9 0.0 copy-start
  29.9 0.0 copy-start.1
  29.9 8.3 %all_to_all.61 = bf16[2,32,64,128]{3,2,1,0:T(8,128)(2,1)S(1)} all-to-all(bf16[2,32,64,128]{3,2,1,0:T(8,128)(2,1)S(1)} %broadcast_in_dim.19), channel_id=1, replica_groups=mesh['island'=4,'fsdp_0'=2,'fsdp_1'=4,'fsdp_2'=4,'fsdp_3'=2] {'fsdp_3'}, dimensions={0} | all-to-all | bytes 2097152 | tf_op jit(solution)/shard_map/all_to_all | solution.py:25
  38.3 0.1 copy.22
  38.3 0.0 copy-done
  38.4 0.0 copy-done.1
  38.4 2.1 fusion.5
  40.5 0.4 convolution_convert_fusion.1
  40.9 3.8 %all_to_all.62 = bf16[2,32,2,128]{3,2,1,0:T(2,128)(2,1)S(1)} all-to-all(bf16[2,32,2,128]{3,2,1,0:T(2,128)(2,1)S(1)} %bitcast.72), channel_id=1, replica_groups=mesh['island'=4,'fsdp_0'=2,'fsdp_1'=4,'fsdp_2'=4,'fsdp_3'=2] {'fsdp_3'}, dimensions={0} | all-to-all | bytes 65536 | tf_op jit(solution)/shard_map/all_to_all | solution.py:57
  44.7 0.6 reduce_sum.66
  45.3 3.8 %all-to-all-start.3 = ((bf16[32,2,128]{2,1,0:T(2,128)(2,1)}), bf16[32,2,128]{2,1,0:T(2,128)(2,1)S(1)}, u32[]{:S(2)}, u32[]{:S(2)}) async-start(bf16[32,2,128]{2,1,0:T(2,128)(2,1)} %reduce_sum.66), calls=%async_computation.3 | async-start | bytes 32768 | tf_op jit(solution)/shard_map/all_to_all | solution.py:65
  49.2 8.2 %convolution_convert_fusion = bf16[4096,128]{1,0:T(8,128)(2,1)S(1)} fusion(f32[224,128]{1,0:T(8,128)S(1)} %fusion.5, bf16[1,224,4096]{2,1,0:T(8,128)(2,1)S(1)} %copy-done, bf16[1,1,224,4096]{3,2,1,0:T(8,128)(2,1)} %param.5), kind=kOutput, calls=%fused_computation.6 | convolution fusion | flops 1412562944 | bytes 4833280 | tf_op jit(solution)/shard_map/dot_general | solution.py:83
  57.4 1.0 copy.32
  58.4 1.7 all-to-all-done.3
  60.2 5.3 %all-to-all-start.6 = ((bf16[2,32,64,128]{3,2,1,0:T(8,128)(2,1)}), bf16[2,32,64,128]{3,2,1,0:T(8,128)(2,1)S(1)}, u32[]{:S(2)}, u32[]{:S(2)}) async-start(bf16[2,32,64,128]{3,2,1,0:T(8,128)(2,1)} %bitcast.67), calls=%async_computation.6 | async-start | bytes 2097152 | tf_op jit(solution)/shard_map/all_to_all | solution.py:57
  65.6 1.7 all-to-all-done.6
  67.3 0.6 broadcast_in_dim.20
  67.9 9.1 %all-to-all-start.4 = ((bf16[32,2,128]{2,1,0:T(2,128)(2,1)}), bf16[32,2,128]{2,1,0:T(2,128)(2,1)S(1)}, u32[]{:S(2)}, u32[]{:S(2)}) async-start(bf16[32,2,128]{2,1,0:T(2,128)(2,1)} %broadcast_in_dim.20), calls=%async_computation.4 | async-start | bytes 32768 | tf_op jit(solution)/shard_map/all_to_all | solution.py:25
  77.0 1.1 reduce_sum.68
  78.1 9.8 %all-to-all-done.4 = bf16[32,2,128]{2,1,0:T(2,128)(2,1)S(1)} async-done(((bf16[32,2,128]{2,1,0:T(2,128)(2,1)}), bf16[32,2,128]{2,1,0:T(2,128)(2,1)S(1)}, u32[]{:S(2)}, u32[]{:S(2)}) %all-to-all-start.4) | async-done | bytes 16416 | tf_op jit(solution)/shard_map/all_to_all | solution.py:25
  88.0 5.4 %all_to_all.63 = bf16[2,32,2,128]{3,2,1,0:T(2,128)(2,1)S(1)} all-to-all(bf16[2,32,2,128]{3,2,1,0:T(2,128)(2,1)S(1)} %broadcast_in_dim.21), channel_id=1, replica_groups=mesh['island'=4,'fsdp_0'=2,'fsdp_1'=4,'fsdp_2'=4,'fsdp_3'=2] {'fsdp_3'}, dimensions={0} | all-to-all | bytes 65536 | tf_op jit(solution)/shard_map/all_to_all | solution.py:25
  93.4 3.9 %all-to-all-start.7 = ((bf16[32,64,128]{2,1,0:T(8,128)(2,1)}), bf16[32,64,128]{2,1,0:T(8,128)(2,1)S(1)}, u32[]{:S(2)}, u32[]{:S(2)}) async-start(bf16[32,64,128]{2,1,0:T(8,128)(2,1)} %reduce_sum.68), calls=%async_computation.7 | async-start | bytes 1048576 | tf_op jit(solution)/shard_map/all_to_all | solution.py:65
  97.3 0.1 copy.26
  97.4 14.0 %all-to-all-done.7 = bf16[32,64,128]{2,1,0:T(8,128)(2,1)S(1)} async-done(((bf16[32,64,128]{2,1,0:T(8,128)(2,1)}), bf16[32,64,128]{2,1,0:T(8,128)(2,1)S(1)}, u32[]{:S(2)}, u32[]{:S(2)}) %all-to-all-start.7) | async-done | bytes 524320 | tf_op jit(solution)/shard_map/all_to_all | solution.py:65
  111.4 0.1 reduce_sum.69
  111.5 0.9 broadcast_in_dim.22
  112.4 4.7 %all-to-all-start.8 = ((bf16[32,64,128]{2,1,0:T(8,128)(2,1)}), bf16[32,64,128]{2,1,0:T(8,128)(2,1)S(1)}, u32[]{:S(2)}, u32[]{:S(2)}) async-start(bf16[32,64,128]{2,1,0:T(8,128)(2,1)} %broadcast_in_dim.22), calls=%async_computation.8 | async-start | bytes 1048576 | tf_op jit(solution)/shard_map/all_to_all | solution.py:25
  117.1 11.7 %cholesky.17 = f32[128,128]{1,0:T(8,128)S(1)} custom-call(f32[128,128]{1,0:T(8,128)S(1)} %fusion.14), custom_call_target="Cholesky" | custom-call | tf_op jit(solution)/shard_map/jit(cholesky)/cholesky | solution.py:119
  128.9 0.6 compare_reduce_fusion
  129.5 0.7 fusion.11
  130.2 9.8 %custom-call.6 = f32[1,128,128]{1,2,0:T(8,128)S(1)} custom-call(f32[1,128,128]{2,1,0:T(8,128)S(1)} %fusion.11), custom_call_target="InvertDiagBlocksLowerTriangular" | custom-call | tf_op jit(solution)/shard_map/triangular_solve | solution.py:94
  140.0 0.2 fusion.12
  140.2 0.2 fusion.15
  140.4 0.0 all-to-all-done.8
  140.5 0.3 broadcast_in_dim.23
  140.7 10.5 %all_to_all.64 = bf16[2,32,64,128]{3,2,1,0:T(8,128)(2,1)S(1)} all-to-all(bf16[2,32,64,128]{3,2,1,0:T(8,128)(2,1)S(1)} %broadcast_in_dim.23), channel_id=1, replica_groups=mesh['island'=4,'fsdp_0'=2,'fsdp_1'=4,'fsdp_2'=4,'fsdp_3'=2] {'fsdp_3'}, dimensions={0} | all-to-all | bytes 2097152 | tf_op jit(solution)/shard_map/all_to_all | solution.py:25
  151.3 0.1 copy.28
  151.4 1.0 multiply_reduce_fusion
  152.4 0.0 copy-start.2
  152.4 4.2 %fusion.1 = bf16[224,4096]{1,0:T(8,128)(2,1)} fusion(f32[224,128]{1,0:T(8,128)S(1)} %fusion.15, f32[4096,128]{1,0:T(8,128)S(1)} %get-tuple-element.6, f32[128]{0:T(128)S(1)} %add_sqrt_fusion), kind=kOutput, calls=%fused_computation.3 | convolution fusion | flops 1411645440 | bytes 4047360 | tf_op jit(solution)/shard_map/dot_general | solution.py:83
  156.6 0.0 copy-done.2
  156.6 4.4 %all-to-all-start.10 = ((bf16[4,56,4096]{2,1,0:T(8,128)(2,1)}), bf16[4,56,4096]{2,1,0:T(8,128)(2,1)}, u32[]{:S(2)}, u32[]{:S(2)}) async-start(bf16[4,56,4096]{2,1,0:T(8,128)(2,1)} %bitcast.69), calls=%async_computation.10 | async-start | bytes 3670016 | tf_op jit(solution)/shard_map/all_to_all | solution.py:57
  161.0 0.0 copy-start.3
  161.0 43.0 %all-to-all-done.10 = bf16[4,56,4096]{2,1,0:T(8,128)(2,1)} async-done(((bf16[4,56,4096]{2,1,0:T(8,128)(2,1)}), bf16[4,56,4096]{2,1,0:T(8,128)(2,1)}, u32[]{:S(2)}, u32[]{:S(2)}) %all-to-all-start.10) | async-done | bytes 1835040 | tf_op jit(solution)/shard_map/all_to_all | solution.py:57
  204.0 1.9 convert_reduce_fusion
  205.9 0.0 copy-done.3
  205.9 2.2 subtract_convert_fusion
  208.1 1.4 broadcast_in_dim.24
  209.6 4.4 %all-to-all-start.11 = ((bf16[4,56,4096]{2,1,0:T(8,128)(2,1)}), bf16[4,56,4096]{2,1,0:T(8,128)(2,1)}, u32[]{:S(2)}, u32[]{:S(2)}) async-start(bf16[4,56,4096]{2,1,0:T(8,128)(2,1)} %broadcast_in_dim.24), calls=%async_computation.11 | async-start | bytes 3670016 | tf_op jit(solution)/shard_map/all_to_all | solution.py:25
  214.0 6.9 %fusion.3 = bf16[1,224,4096]{2,1,0:T(8,128)(2,1)} fusion(f32[224,128]{1,0:T(8,128)S(1)} %fusion.15, f32[4096,128]{1,0:T(8,128)} %copy-done.2, bf16[1,1,224,4096]{3,2,1,0:T(8,128)(2,1)} %param.5, bf16[1,224,4096]{2,1,0:T(8,128)(2,1)S(1)} %copy-done), kind=kOutput, calls=%fused_computation.5 | convolution fusion | flops 1414791168 | bytes 7716864 | tf_op jit(solution)/shard_map/dot_general | solution.py:83
  220.9 35.3 %all-to-all-done.11 = bf16[4,56,4096]{2,1,0:T(8,128)(2,1)} async-done(((bf16[4,56,4096]{2,1,0:T(8,128)(2,1)}), bf16[4,56,4096]{2,1,0:T(8,128)(2,1)}, u32[]{:S(2)}, u32[]{:S(2)}) %all-to-all-start.11) | async-done | bytes 1835040 | tf_op jit(solution)/shard_map/all_to_all | solution.py:25
  256.2 2.9 %copy.35 = bf16[224,4096]{1,0:T(8,128)(2,1)} copy(bf16[224,4096]{1,0:T(8,128)(2,1)} %bitcast.19) | data formatting | bytes 3670016
  (8 shorter events, 0.2 us)
Async XLA Ops:
  29.9 8.5 %copy-start = (bf16[1,224,4096]{2,1,0:T(8,128)(2,1)S(1)}, bf16[1,224,4096]{2,1,0:T(8,128)(2,1)}, u32[]{:S(2)}) copy-start(bf16[1,224,4096]{2,1,0:T(8,128)(2,1)} %param.6) | copy-start | bytes 5505028
  29.9 8.5 %copy-start.1 = (bf16[1,1,224,4096]{3,2,1,0:T(8,128)(2,1)S(1)}, bf16[1,1,224,4096]{3,2,1,0:T(8,128)(2,1)}, u32[]{:S(2)}) copy-start(bf16[1,1,224,4096]{3,2,1,0:T(8,128)(2,1)} %param.5) | copy-start | bytes 5505028
  45.3 14.8 %all-to-all-start.3 = ((bf16[32,2,128]{2,1,0:T(2,128)(2,1)}), bf16[32,2,128]{2,1,0:T(2,128)(2,1)S(1)}, u32[]{:S(2)}, u32[]{:S(2)}) async-start(bf16[32,2,128]{2,1,0:T(2,128)(2,1)} %reduce_sum.66), calls=%async_computation.3 | async-start | bytes 32768 | tf_op jit(solution)/shard_map/all_to_all | solution.py:65
  60.2 7.1 %all-to-all-start.6 = ((bf16[2,32,64,128]{3,2,1,0:T(8,128)(2,1)}), bf16[2,32,64,128]{3,2,1,0:T(8,128)(2,1)S(1)}, u32[]{:S(2)}, u32[]{:S(2)}) async-start(bf16[2,32,64,128]{3,2,1,0:T(8,128)(2,1)} %bitcast.67), calls=%async_computation.6 | async-start | bytes 2097152 | tf_op jit(solution)/shard_map/all_to_all | solution.py:57
  67.9 20.1 %all-to-all-start.4 = ((bf16[32,2,128]{2,1,0:T(2,128)(2,1)}), bf16[32,2,128]{2,1,0:T(2,128)(2,1)S(1)}, u32[]{:S(2)}, u32[]{:S(2)}) async-start(bf16[32,2,128]{2,1,0:T(2,128)(2,1)} %broadcast_in_dim.20), calls=%async_computation.4 | async-start | bytes 32768 | tf_op jit(solution)/shard_map/all_to_all | solution.py:25
  93.4 18.1 %all-to-all-start.7 = ((bf16[32,64,128]{2,1,0:T(8,128)(2,1)}), bf16[32,64,128]{2,1,0:T(8,128)(2,1)S(1)}, u32[]{:S(2)}, u32[]{:S(2)}) async-start(bf16[32,64,128]{2,1,0:T(8,128)(2,1)} %reduce_sum.68), calls=%async_computation.7 | async-start | bytes 1048576 | tf_op jit(solution)/shard_map/all_to_all | solution.py:65
  112.4 28.0 %all-to-all-start.8 = ((bf16[32,64,128]{2,1,0:T(8,128)(2,1)}), bf16[32,64,128]{2,1,0:T(8,128)(2,1)S(1)}, u32[]{:S(2)}, u32[]{:S(2)}) async-start(bf16[32,64,128]{2,1,0:T(8,128)(2,1)} %broadcast_in_dim.22), calls=%async_computation.8 | async-start | bytes 1048576 | tf_op jit(solution)/shard_map/all_to_all | solution.py:25
  152.4 4.3 %copy-start.2 = (f32[4096,128]{1,0:T(8,128)}, f32[4096,128]{1,0:T(8,128)S(1)}, u32[]{:S(2)}) copy-start(f32[4096,128]{1,0:T(8,128)S(1)} %get-tuple-element.6) | copy-start | bytes 6291460
  156.6 47.4 %all-to-all-start.10 = ((bf16[4,56,4096]{2,1,0:T(8,128)(2,1)}), bf16[4,56,4096]{2,1,0:T(8,128)(2,1)}, u32[]{:S(2)}, u32[]{:S(2)}) async-start(bf16[4,56,4096]{2,1,0:T(8,128)(2,1)} %bitcast.69), calls=%async_computation.10 | async-start | bytes 3670016 | tf_op jit(solution)/shard_map/all_to_all | solution.py:57
  161.0 44.9 %copy-start.3 = (f32[56,4096]{1,0:T(8,128)S(1)}, f32[56,4096]{1,0:T(8,128)}, u32[]{:S(2)}) copy-start(f32[56,4096]{1,0:T(8,128)} %param.9) | copy-start | bytes 2752516
  209.6 46.6 %all-to-all-start.11 = ((bf16[4,56,4096]{2,1,0:T(8,128)(2,1)}), bf16[4,56,4096]{2,1,0:T(8,128)(2,1)}, u32[]{:S(2)}, u32[]{:S(2)}) async-start(bf16[4,56,4096]{2,1,0:T(8,128)(2,1)} %broadcast_in_dim.24), calls=%async_computation.11 | async-start | bytes 3670016 | tf_op jit(solution)/shard_map/all_to_all | solution.py:25
where the time goes:
time: 260 us; the launch traced here: 259 us
  waiting for transfers between devices  106 us (41%)
  blocking collectives  56.1 us (22%)
  starting transfers between devices  35.6 us (14%)
  other arithmetic  29.7 us (11%)
  matrix products  23.3 us (9%)
  local copies, waits for them, and re-layouts  7.96 us (3%)
    all_to_all x4, blocking collectives, from_everyone(): lax.all_to_all(jnp.broadcast_to(shard[None], (devices, *shard.shape)), ax...  52.3 us
    all_to_all x3, waiting for transfers between devices, from_everyone(): lax.all_to_all(jnp.broadcast_to(shard[None], (devices, *shard.shape)), ax...  45.2 us
    all_to_all x2, waiting for transfers between devices, sent_and_summed(): lax.all_to_all(split_up(shard, dim, devices), axis, 0, 0, tiled=True)  44.7 us
    dot_general x7, matrix products, product(): lax.dot_general(left_side, right_side, (((left_dims,), (right_dims,)), ((...  23.1 us
    all_to_all x3, starting transfers between devices, from_everyone(): lax.all_to_all(jnp.broadcast_to(shard[None], (devices, *shard.shape)), ax...  18.1 us
    all_to_all x2, waiting for transfers between devices, sum_by_axis(): lax.all_to_all(nearer.astype(jnp.bfloat16), far, split_axis=0, concat_axi...  15.8 us
    another operation x3, other arithmetic, body(): upper_inverse = inverse_upper(jnp.linalg.cholesky(gram_matrix))  12.4 us
    another operation x2, other arithmetic, inverse_upper(): lax.linalg.triangular_solve(lower_factor, identity, left_side=True, lower...  10.5 us
  transfers between devices with their start and end apart: 7, of which 6 were waited for; matrix products, arithmetic and copies ran while one was open for 16% of the time, Pallas kernels for 0%

commit v1 on v0

v1 whole, which is shorter than its diff:
```python
import math

import jax
import jax.numpy as jnp
from jax import lax
from jax.experimental import pallas as pl
from jax.experimental.pallas import tpu as pltpu
from jax.sharding import Mesh
from jax.sharding import PartitionSpec as P

ROWS = 14336
COLS = 4096
RANK = 128
FSDP = ("fsdp_0", "fsdp_1", "fsdp_2", "fsdp_3")
FSDP_ISLAND = ("fsdp_0", "fsdp_1", "fsdp_2", "fsdp_3", "island")
OWN = 224
PADDED = 256
QUARTER = 56
QUARTER_PADDED = 64
STEP_COLS = 512
MESH = pl.DeviceIdType.MESH

precise = lax.Precision.HIGHEST
error_decay = 0.95
outer_beta = 0.9
outer_rate = 0.7
epsilon = 1e-06
f32 = jnp.float32
bf16 = jnp.bfloat16


def dot(left, right, left_dim, right_dim, precision=None):
    return lax.dot_general(
        left,
        right,
        (((left_dim,), (right_dim,)), ((), ())),
        precision=precision,
        preferred_element_type=f32,
    )


def inverse_lower(gram, width=2):
    n = gram.shape[0]
    rest = gram
    side = (
        lax.broadcasted_iota(jnp.int32, (n, n), 0) == lax.broadcasted_iota(jnp.int32, (n, n), 1)
    ).astype(f32)
    done = []
    for first in range(0, n, 8):
        rows = lax.broadcasted_iota(jnp.int32, rest.shape, 0)
        scale = jnp.ones((8, n), f32)
        head = lax.broadcasted_iota(jnp.int32, (8, n), 0)
        for at in range(0, 8, width):
            columns = [
                jnp.broadcast_to(rest[:, first + at + i : first + at + i + 1], rest.shape)
                for i in range(width)
            ]
            for i in range(width):
                row = at + i
                pivot = columns[i][row : row + 1, :]
                times = jnp.where(rows > row, columns[i] * (1.0 / pivot), 0.0)
                scale = jnp.where(head == row, pivot, scale)
                for j in range(i + 1, width):
                    columns[j] = columns[j] - times * columns[j][row : row + 1, :]
                rest = rest - times * rest[row : row + 1, :]
                side = side - times * side[row : row + 1, :]
        done.append(side[:8] * lax.rsqrt(scale))
        rest, side = rest[8:], side[8:]
    return jnp.concatenate(done, axis=0)


def exchange_kernel(
    grads,
    buffer,
    q_old,
    momentum,
    f_all,
    p_scaled,
    p_own,
    mom_all,
    grads_v,
    buffer_v,
    mom_v,
    mb,
    qa,
    raw_b,
    gsend,
    g1,
    g2,
    g3,
    g4,
    gfull,
    rp,
    rown,
    r1,
    s1,
    r2,
    s2,
    s2b,
    r3,
    s3b,
    r4,
    p_all,
    squares,
    load_sem,
    send_sem,
    recv_sem,
):
    c = lax.axis_index("island")
    h = lax.axis_index("fsdp_0")
    x = lax.axis_index("fsdp_1")
    y = lax.axis_index("fsdp_2")
    k = lax.axis_index("fsdp_3")
    z = h * 4 + c
    a = x * (1 - k) + y * k
    b = y * (1 - k) + x * k

    def first_axis(d):
        return {"fsdp_1": lax.rem(x + d * (1 - k), 4), "fsdp_2": lax.rem(y + d * k, 4)}

    def second_axis(d):
        return {"fsdp_1": lax.rem(x + d * k, 4), "fsdp_2": lax.rem(y + d * (1 - k), 4)}

    def along_z(d):
        to = lax.rem(z + d, 8)
        return {"fsdp_0": to // 4, "island": lax.rem(to, 4)}

    other_core = {"fsdp_3": 1 - k}
    other_half = {"fsdp_0": 1 - h}

    peers = [other_core, other_half]
    for d in (1, 2, 3):
        peers.append({"fsdp_1": lax.rem(x + d, 4)})
        peers.append({"fsdp_2": lax.rem(y + d, 4)})
        peers.append({"fsdp_0": 1 - h, "fsdp_1": lax.rem(x + d, 4)})
        peers.append({"island": lax.rem(c + d, 4)})
    for d in (1, 2, 6, 7):
        peers.append(along_z(d))

    counter = [0]
    started = []

    def copy_to(src, dst, device):
        at = counter[0]
        counter[0] += 1
        copy = pltpu.make_async_remote_copy(
            src_ref=src,
            dst_ref=dst,
            send_sem=send_sem.at[at],
            recv_sem=recv_sem.at[at],
            device_id=device,
            device_id_type=MESH,
        )
        return copy

    def send(src, dst, device):
        copy = copy_to(src, dst, device)
        copy.start()
        started.append(copy)
        return copy

    barrier = pltpu.get_barrier_semaphore()
    for peer in peers:
        pl.semaphore_signal(barrier, inc=1, device_id=peer, device_id_type=MESH)

    loads = [
        pltpu.make_async_copy(momentum, mom_v, load_sem.at[0]),
        pltpu.make_async_copy(grads, grads_v, load_sem.at[1]),
        pltpu.make_async_copy(buffer, buffer_v, load_sem.at[2]),
    ]
    for load in loads:
        load.start()
    qa[h, x, y, k] = q_old[...].astype(bf16)
    loads[0].wait()
    mom_all[c] = jnp.concatenate(
        [mom_v[...], jnp.zeros((QUARTER_PADDED - QUARTER, COLS), f32)], axis=0
    ).astype(bf16)
    pl.semaphore_wait(barrier, len(peers))

    own_piece = qa.at[h, x, y, k]
    q_copies = {}
    for dh in (0, 1):
        for dx in (1, 2, 3) if dh == 0 else (0, 1, 2, 3):
            q_copies[dh, dx] = send(
                own_piece,
                own_piece,
                {"fsdp_0": lax.rem(h + dh, 2), "fsdp_1": lax.rem(x + dx, 4)},
            )

    line = []
    for step in (1, 2, 3):
        up_ok = jnp.logical_and(c < 3, c >= step - 1)
        down_ok = jnp.logical_and(c > 0, c + step - 1 <= 3)
        up_at = lax.rem(c - (step - 1) + 4, 4)
        down_at = lax.rem(c + (step - 1), 4)
        up = copy_to(mom_all.at[up_at], mom_all.at[up_at], {"island": lax.rem(c + 1, 4)})
        down = copy_to(mom_all.at[down_at], mom_all.at[down_at], {"island": lax.rem(c + 3, 4)})
        line.append((up_ok, up, c - step >= 0, down_ok, down, c + step <= 3))

    def line_send(step):
        up_ok, up, _, down_ok, down, _ = line[step - 1]

        @pl.when(up_ok)
        def _():
            up.start()

        @pl.when(down_ok)
        def _():
            down.start()

    def line_receive(step):
        up_ok, up, from_below, down_ok, down, from_above = line[step - 1]

        @pl.when(from_below)
        def _():
            up.wait_recv()

        @pl.when(from_above)
        def _():
            down.wait_recv()

        @pl.when(up_ok)
        def _():
            up.wait_send()

        @pl.when(down_ok)
        def _():
            down.wait_send()

    line_send(1)

    loads[1].wait()
    loads[2].wait()

    @pl.loop(0, OWN // 16)
    def _(i):
        at = pl.ds(pl.multiple_of(i * 16, 16), 16)
        mb[at, :] = (grads_v[at, :].astype(f32) + buffer_v[at, :].astype(f32)).astype(bf16)

    mb[OWN:, :] = jnp.zeros((PADDED - OWN, COLS), bf16)

    up_y = {"fsdp_2": lax.rem(y + 1, 4)}
    down_y = {"fsdp_2": lax.rem(y + 3, 4)}
    below, above = lax.rem(y + 3, 4), lax.rem(y + 1, 4)
    q_ring = []
    for group in (0, 1):
        at = lax.rem(h + group, 2)
        for dx in (1, 2, 3) if group == 0 else (0, 1, 2, 3):
            q_copies[group, dx].wait_recv()
        mine = qa.at[at, :, y, k]
        q_ring.append((at, send(mine, mine, up_y), send(mine, mine, down_y)))
    q_forward = []
    for at, up, down in q_ring:
        up.wait_recv()
        came = qa.at[at, 0:2, below, k]
        on_up = send(came, came, up_y)
        down.wait_recv()
        came = qa.at[at, 2:4, above, k]
        on_down = send(came, came, down_y)
        q_forward.append((at, on_up, on_down))
    q_cross = []
    for at, on_up, on_down in q_forward:
        on_up.wait_recv()
        on_down.wait_recv()
        half = qa.at[at, :, :, k]
        q_cross.append((at, send(half, half, other_core)))

    raw = jnp.zeros((PADDED, RANK), f32)
    for at, copy in q_cross:
        copy.wait_recv()
        columns = pl.ds(pl.multiple_of(at * (COLS // 2), COLS // 2), COLS // 2)
        raw = raw + dot(mb[:, columns], qa[at].reshape(COLS // 2, RANK), 1, 0)
    raw_b[...] = raw.astype(bf16)
    raw_rows = raw_b[...]

    gram = dot(raw_rows, raw_rows, 0, 0)
    gsend[0] = gram[:64]
    gsend[1] = gram[64:]
    gram_cross = send(gsend.at[1 - k], g1, other_core)

    raw_t = raw.T.astype(bf16)

    def image(half, part, store):
        columns = pl.ds(pl.multiple_of(half * (COLS // 2) + part * 256, 256), 256)
        block = dot(raw_t, mb[:, columns], 1, 0)
        store(part * 2, block[:, :128])
        store(part * 2 + 1, block[:, 128:])

    def store_far(at, block):
        rp[at] = block.astype(bf16)

    def store_near(at, block):
        rown[at] = block

    r_cross = []
    for chunk in (0, 1):
        for part in range(chunk * 4, chunk * 4 + 4):
            image(1 - k, part, store_far)
        piece = pl.ds(chunk * 8, 8)
        r_cross.append(send(rp.at[piece], r1.at[piece], other_core))

    gram_cross.wait_recv()
    g2[a] = gsend[k] + g1[...]
    gram_first = [send(g2.at[a], g2.at[a], first_axis(d)) for d in (2, 1, 3)]

    for part in range(8):
        image(k, part, store_near)

    for copy in r_cross:
        copy.wait_recv()
    r_first = []
    for d in (2, 1, 3):
        to = lax.rem(a + d, 4)
        for j in range(4):
            s1[d - 1, j] = (rown[to * 4 + j] + r1[to * 4 + j].astype(f32)).astype(bf16)
        r_first.append(send(s1.at[d - 1], r2.at[d - 1], first_axis(d)))

    line_receive(1)
    line_send(2)

    for copy in gram_first:
        copy.wait_recv()
    g3[b] = (g2[0] + g2[1]) + (g2[2] + g2[3])
    gram_second = [send(g3.at[b], g3.at[b], second_axis(d)) for d in (2, 1, 3)]

    for copy in r_first:
        copy.wait_recv()
    for j in range(4):
        s2[j] = (rown[a * 4 + j] + r1[a * 4 + j].astype(f32)) + (
            (r2[0, j].astype(f32) + r2[1, j].astype(f32)) + r2[2, j].astype(f32)
        )
    r_second = []
    for d in (2, 1, 3):
        s2b[d - 1] = s2[lax.rem(b + d, 4)].astype(bf16)
        r_second.append(send(s2b.at[d - 1], r3.at[d - 1], second_axis(d)))

    for copy in gram_second:
        copy.wait_recv()
    g4[h] = (g3[0] + g3[1]) + (g3[2] + g3[3])
    gram_third = send(g4.at[h], g4.at[h], other_half)

    for copy in r_second:
        copy.wait_recv()
    s3b[...] = (
        s2[b] + ((r3[0].astype(f32) + r3[1].astype(f32)) + r3[2].astype(f32))
    ).astype(bf16)
    r_third = send(s3b, r4, other_half)

    gram_third.wait_recv()
    gfull[k] = g4[0] + g4[1]
    gram_last = send(gfull.at[k], gfull.at[k], other_core)
    line_receive(2)
    line_send(3)
    gram_last.wait_recv()
    lower = inverse_lower(jnp.concatenate([gfull[0], gfull[1]], axis=0))

    r_third.wait_recv()
    image_sum = s3b[...].astype(f32) + r4[...].astype(f32)
    f_all[k, a, b, c] = dot(lower, image_sum, 1, 0, precise).astype(bf16)

    mine = f_all.at[k, a, b, c]
    z_copies = [send(mine, mine, along_z(d)) for d in (2, 1, 7)]
    basis = dot(raw_rows.astype(f32), lower, 1, 1, precise)[:OWN]
    p_all[c] = basis.astype(bf16)
    p_copies = [send(p_all.at[c], p_all.at[c], {"island": lax.rem(c + d, 4)}) for d in (1, 2, 3)]
    p_own[...] = (basis * (error_decay - 1.0)).astype(bf16)

    up_a, down_a = first_axis(1), first_axis(3)
    up_b, down_b = second_axis(1), second_axis(3)
    a_below, a_above = lax.rem(a + 3, 4), lax.rem(a + 1, 4)
    b_below, b_above, b_far = lax.rem(b + 3, 4), lax.rem(b + 1, 4), lax.rem(b + 2, 4)

    def ring_a(at):
        piece = f_all.at[k, a, at]
        return (at, send(piece, piece, up_a), send(piece, piece, down_a))

    def forward_a(ring):
        at, up, down = ring
        up.wait_recv()
        came = f_all.at[k, a_below, at, 0:2]
        on_up = send(came, came, up_a)
        down.wait_recv()
        came = f_all.at[k, a_above, at, 2:4]
        on_down = send(came, came, down_a)
        return (at, on_up, on_down)

    def cross(ring):
        at, on_up, on_down = ring
        on_up.wait_recv()
        on_down.wait_recv()
        part = f_all.at[k, :, at]
        return send(part, part, other_core)

    for copy in z_copies:
        copy.wait_recv()
    piece = f_all.at[k, a, b]
    up, down = send(piece, piece, up_b), send(piece, piece, down_b)
    ring_own = ring_a(b)
    up.wait_recv()
    came = f_all.at[k, a, b_below, 0:2]
    on_up = send(came, came, up_b)
    down.wait_recv()
    came = f_all.at[k, a, b_above, 2:4]
    on_down = send(came, came, down_b)
    ring_below = ring_a(b_below)
    ring_above = ring_a(b_above)
    own_on = forward_a(ring_own)
    on_up.wait_recv()
    on_down.wait_recv()
    ring_far = ring_a(b_far)
    below_on = forward_a(ring_below)
    above_on = forward_a(ring_above)
    crossing = [cross(own_on)]
    far_on = forward_a(ring_far)
    crossing.append(cross(below_on))
    crossing.append(cross(above_on))
    line_receive(3)
    crossing.append(cross(far_on))
    for copy in crossing:
        copy.wait_recv()

    squares[...] = jnp.zeros_like(squares)

    @pl.loop(0, 8)
    def _(i):
        for j in range(4):
            for island in range(4):
                values = f_all[i // 4, lax.rem(i, 4), j, island].astype(f32)
                squares[island] += values * values

    ones = jnp.ones((8, RANK), f32)
    for copy in p_copies:
        copy.wait_recv()
    rate = math.sqrt(ROWS * COLS / RANK) / 4.0
    for island in range(4):
        total = dot(ones, squares[island], 1, 1, precise)[:1]
        scale = rate * lax.rsqrt(total + epsilon)
        p_scaled[:, island * RANK : (island + 1) * RANK] = (
            p_all[island].astype(f32) * scale
        ).astype(bf16)
    for copy in started:
        copy.wait_send()


def exchange(grads, buffer, q_old, momentum):
    vmem = pltpu.VMEM
    whole = pl.BlockSpec(memory_space=pltpu.VMEM)
    anywhere = pl.BlockSpec(memory_space=pl.ANY)
    block = (128, 128)
    return pl.pallas_call(
        exchange_kernel,
        out_shape=(
            jax.ShapeDtypeStruct((2, 4, 4, 4, 128, 128), bf16),
            jax.ShapeDtypeStruct((OWN, 4 * RANK), bf16),
            jax.ShapeDtypeStruct((OWN, RANK), bf16),
            jax.ShapeDtypeStruct((4, QUARTER_PADDED, COLS), bf16),
        ),
        in_specs=[anywhere, anywhere, whole, anywhere],
        out_specs=(whole, whole, whole, whole),
        scratch_shapes=[
            vmem((OWN, COLS), bf16),
            vmem((OWN, COLS), bf16),
            vmem((QUARTER, COLS), f32),
            vmem((PADDED, COLS), bf16),
            vmem((2, 4, 4, 2, 64, RANK), bf16),
            vmem((PADDED, RANK), bf16),
            vmem((2, 64, 128), f32),
            vmem((64, 128), f32),
            vmem((4, 64, 128), f32),
            vmem((4, 64, 128), f32),
            vmem((2, 64, 128), f32),
            vmem((2, 64, 128), f32),
            vmem((16, *block), bf16),
            vmem((16, *block), f32),
            vmem((16, *block), bf16),
            vmem((3, 4, *block), bf16),
            vmem((3, 4, *block), bf16),
            vmem((4, *block), f32),
            vmem((3, *block), bf16),
            vmem((3, *block), bf16),
            vmem(block, bf16),
            vmem(block, bf16),
            vmem((4, OWN, RANK), bf16),
            vmem((4, *block), f32),
            pltpu.SemaphoreType.DMA((3,)),
            pltpu.SemaphoreType.DMA((80,)),
            pltpu.SemaphoreType.DMA((80,)),
        ],
        compiler_params=pltpu.CompilerParams(collective_id=0, has_side_effects=True),
        name="exchange",
    )(grads, buffer, q_old, momentum)


def update_kernel(
    factors, p_scaled, p_own, mom_all, grads, buffer, anchor, momentum, anchor_new, buffer_new, momentum_new, means
):
    c = lax.axis_index("island")
    pieces = STEP_COLS // 128
    for pair in range(0, pieces, 2):
        at = slice(pair * 128, pair * 128 + 256)
        both = jnp.concatenate(
            [factors[pair + i].reshape(4 * RANK, 128) for i in (0, 1)], axis=1
        )
        means[:, at] = dot(p_scaled[...], both, 1, 0)
        own = jnp.concatenate([factors[pair + i, c] for i in (0, 1)], axis=1)
        matrix = grads[:, at].astype(f32) + buffer[:, at].astype(f32)
        buffer_new[:, at] = (matrix + dot(p_own[...], own, 1, 0)).astype(bf16)
    carried = jnp.concatenate(
        [mom_all[i].astype(f32)[:QUARTER] for i in range(4)], axis=0
    )
    mean = means[...]
    anchor_new[...] = (
        anchor[...].astype(f32)
        - outer_rate * (mean + outer_beta * (outer_beta * carried + mean))
    ).astype(bf16)
    rows = pl.ds(pl.multiple_of(c * QUARTER, 8), QUARTER)
    momentum_new[...] = outer_beta * momentum[...] + means[rows, :]


def update(factors, p_scaled, p_own, mom_all, grads, buffer, anchor, momentum):
    wide = pl.BlockSpec((OWN, STEP_COLS), lambda i: (0, i))
    narrow = pl.BlockSpec((QUARTER, STEP_COLS), lambda i: (0, i))
    return pl.pallas_call(
        update_kernel,
        grid=(COLS // STEP_COLS,),
        out_shape=(
            jax.ShapeDtypeStruct((OWN, COLS), bf16),
            jax.ShapeDtypeStruct((OWN, COLS), bf16),
            jax.ShapeDtypeStruct((QUARTER, COLS), f32),
        ),
        in_specs=[
            pl.BlockSpec((STEP_COLS // 128, 4, 128, 128), lambda i: (i, 0, 0, 0)),
            pl.BlockSpec((OWN, 4 * RANK), lambda i: (0, 0)),
            pl.BlockSpec((OWN, RANK), lambda i: (0, 0)),
            pl.BlockSpec((4, QUARTER_PADDED, STEP_COLS), lambda i: (0, 0, i)),
            wide,
            wide,
            wide,
            narrow,
        ],
        out_specs=(wide, wide, narrow),
        scratch_shapes=[pltpu.VMEM((OWN, STEP_COLS), f32)],
        name="update",
    )(factors, p_scaled, p_own, mom_all, grads, buffer, anchor, momentum)


def body(grads, buffer, q_old, anchor, momentum):
    grads, buffer = grads[0, 0], buffer[0]
    f_all, p_scaled, p_own, mom_all = exchange(grads, buffer, q_old[0], momentum)
    factors = f_all.reshape(COLS // 128, 4, 128, 128)
    anchor_new, buffer_new, momentum_new = update(
        factors, p_scaled, p_own, mom_all, grads, buffer, anchor, momentum
    )
    return (anchor_new, buffer_new[None], momentum_new)


def solution(mesh):
    split = Mesh(
        mesh.devices.reshape(mesh.shape["island"], 2, 4, 4, 2),
        ("island", "fsdp_0", "fsdp_1", "fsdp_2", "fsdp_3"),
    )
    return jax.shard_map(
        body,
        mesh=split,
        in_specs=(
            P("island", None, FSDP, None),
            P("island", FSDP, None),
            P("island", FSDP, None),
            P(FSDP, None),
            P(FSDP_ISLAND, None),
        ),
        out_specs=(P(FSDP, None), P("island", FSDP, None), P(FSDP_ISLAND, None)),
        check_vma=False,
    )
```

time: 260 us -> 97.5 us (0.38)
  waiting for transfers between devices: 106 us -> 0 us
  Pallas kernels: 0 us -> 96.6 us
  blocking collectives: 56.1 us -> 0 us
  starting transfers between devices: 35.6 us -> 0 us
  other arithmetic: 29.7 us -> 0 us
  matrix products: 23.3 us -> 0 us
  local copies, waits for them, and re-layouts: 7.96 us -> 0 us
    all_to_all x7 -> x0, waiting for transfers between devices: 106 us -> none  [the longest x3 45.2 us: from_everyone(): lax.all_to_all(jnp.broadcast_to(shard[None], (devices, *shard.shape)), ax...]
    pallas_call x0 -> x2, Pallas kernels: none -> 96.6 us  [the longest x1 86.5 us: exchange(): pl.pallas_call(exchange_kernel, out_shape=(jax.ShapeDtypeStruct((2, 4, 4,...]
    all_to_all x5 -> x0, blocking collectives: 56.1 us -> none  [the longest x4 52.3 us: from_everyone(): lax.all_to_all(jnp.broadcast_to(shard[None], (devices, *shard.shape)), ax...]
    all_to_all x7 -> x0, starting transfers between devices: 35.6 us -> none  [the longest x3 18.1 us: from_everyone(): lax.all_to_all(jnp.broadcast_to(shard[None], (devices, *shard.shape)), ax...]
    dot_general x7 -> x0, matrix products: 23.1 us -> none  [product(): lax.dot_general(left_side, right_side, (((left_dims,), (right_dims,)), ((...]
    another operation x5 -> x0, other arithmetic: 22.9 us -> none  [the longest x3 12.4 us: body(): upper_inverse = inverse_upper(jnp.linalg.cholesky(gram_matrix))]
    reduce_sum x5 -> x0, other arithmetic: 3.81 us -> none  [the longest x3 3.68 us: sent_and_summed(): return jnp.sum(tiles.astype(jnp.float32), axis=0)]
    broadcast_in_dim x7 -> x0, local copies, waits for them, and re-layouts: 3.67 us -> none  [from_everyone(): jnp.broadcast_to(shard[None], (devices, *shard.shape))]
  transfers between devices with their start and end apart: 7 -> 0, of which waited for: 6 -> 0; matrix products, arithmetic and copies ran while one was open for 16% -> 0% of each run, Pallas kernels for 0% -> 0%
where the time goes in v1:
time: 97.5 us; the launch traced here: 97.2 us
  Pallas kernels  96.6 us (99%)
    pallas_call x1, Pallas kernels, exchange(): pl.pallas_call(exchange_kernel, out_shape=(jax.ShapeDtypeStruct((2, 4, 4,...  86.5 us
    pallas_call x1, Pallas kernels, update(): pl.pallas_call(update_kernel, grid=(COLS // STEP_COLS,), out_shape=(jax.S...  10.1 us

profile of v1, /device:TPU:1, one launch (start us, length us, event | category | flops | bytes accessed | tf_op | source)
XLA Modules:
  0.0 97.2 jit_solution(13717664186586268733)
XLA Ops:
  0.6 86.5 %exchange.1 = (bf16[2,4,4,4,128,128]{5,4,3,2,1,0:T(8,128)(2,1)}, bf16[224,512]{1,0:T(8,128)(2,1)}, bf16[224,128]{1,0:T(8,128)(2,1)}, bf16[4,64,4096]{2,1,0:T(8,128)(2,1)}) custom-call(bf16[224,4096]{1,0:T(8,128)(2,1)} %bitcast.5, bf16[224,4096]{1,0:T(8,128)(2,1)} %bitcast.7, f32[64,128]{1,0:T(8,128)} %bitcast.10, f32[56,4096]{1,0:T(8,128)} %momentum.3), custom_call_target="tpu_custom_call" | custom-call | tf_op jit(solution)/shard_map/exchange/pallas_call | solution.py:450
  87.2 10.1 %update.1 = (bf16[224,4096]{1,0:T(8,128)(2,1)}, bf16[224,4096]{1,0:T(8,128)(2,1)}, f32[56,4096]{1,0:T(8,128)}) custom-call(bf16[32,4,128,128]{3,2,1,0:T(8,128)(2,1)} %bitcast.9, bf16[224,512]{1,0:T(8,128)(2,1)} %get-tuple-element.11.p_scaled, bf16[224,128]{1,0:T(8,128)(2,1)} %get-tuple-element.12.p_own, bf16[4,64,4096]{2,1,0:T(8,128)(2,1)} %get-tuple-element.13.mom_all, ...), custom_call_target="tpu_custom_call" | custom-call | tf_op jit(solution)/shard_map/update/pallas_call | solution.py:523

commit v2 on v1

--- a/solution.py
+++ b/solution.py
@@ -16,8 +16,6 @@
 OWN = 224
 PADDED = 256
 QUARTER = 56
-QUARTER_PADDED = 64
-STEP_COLS = 512
 MESH = pl.DeviceIdType.MESH
 
 precise = lax.Precision.HIGHEST
@@ -39,7 +37,7 @@
     )
 
 
-def inverse_lower(gram, width=2):
+def inverse_lower(gram, width=8):
     n = gram.shape[0]
     rest = gram
     side = (
@@ -73,11 +71,21 @@
     grads,
     buffer,
     q_old,
+    anchor,
     momentum,
+    anchor_new,
+    buffer_new,
+    momentum_new,
     f_all,
     p_scaled,
     p_own,
     mom_all,
+    anchor_v,
+    means,
+    nb,
+    na,
+    nk,
+    q_v,
     grads_v,
     buffer_v,
     mom_v,
@@ -101,7 +109,6 @@
     s3b,
     r4,
     p_all,
-    squares,
     load_sem,
     send_sem,
     recv_sem,
@@ -167,14 +174,15 @@
         pltpu.make_async_copy(momentum, mom_v, load_sem.at[0]),
         pltpu.make_async_copy(grads, grads_v, load_sem.at[1]),
         pltpu.make_async_copy(buffer, buffer_v, load_sem.at[2]),
+        pltpu.make_async_copy(anchor, anchor_v, load_sem.at[3]),
+        pltpu.make_async_copy(q_old, q_v, load_sem.at[4]),
     ]
-    for load in loads:
-        load.start()
-    qa[h, x, y, k] = q_old[...].astype(bf16)
+    for at in (4, 0, 1, 2, 3):
+        loads[at].start()
+    loads[4].wait()
+    qa[h, x, y, k] = q_v[...].astype(bf16)
     loads[0].wait()
-    mom_all[c] = jnp.concatenate(
-        [mom_v[...], jnp.zeros((QUARTER_PADDED - QUARTER, COLS), f32)], axis=0
-    ).astype(bf16)
+    mom_all[c] = mom_v[...].astype(bf16)
     pl.semaphore_wait(barrier, len(peers))
 
     own_piece = qa.at[h, x, y, k]
@@ -265,6 +273,8 @@
         half = qa.at[at, :, :, k]
         q_cross.append((at, send(half, half, other_core)))
 
+    line_receive(1)
+    line_send(2)
     raw = jnp.zeros((PADDED, RANK), f32)
     for at, copy in q_cross:
         copy.wait_recv()
@@ -314,9 +324,6 @@
         for j in range(4):
             s1[d - 1, j] = (rown[to * 4 + j] + r1[to * 4 + j].astype(f32)).astype(bf16)
         r_first.append(send(s1.at[d - 1], r2.at[d - 1], first_axis(d)))
-
-    line_receive(1)
-    line_send(2)
 
     for copy in gram_first:
         copy.wait_recv()
@@ -349,16 +356,19 @@
     gram_third.wait_recv()
     gfull[k] = g4[0] + g4[1]
     gram_last = send(gfull.at[k], gfull.at[k], other_core)
-    line_receive(2)
-    line_send(3)
     gram_last.wait_recv()
     lower = inverse_lower(jnp.concatenate([gfull[0], gfull[1]], axis=0))
 
     r_third.wait_recv()
     image_sum = s3b[...].astype(f32) + r4[...].astype(f32)
-    f_all[k, a, b, c] = dot(lower, image_sum, 1, 0, precise).astype(bf16)
+    factor = dot(lower, image_sum, 1, 0, precise).astype(bf16)
+    f_all[k, a, b, c] = factor
+    squared = jnp.square(factor.astype(f32))
+    nb[b, c] = dot(jnp.ones((8, RANK), f32), squared, 1, 1, precise)
 
     mine = f_all.at[k, a, b, c]
+    square = nb.at[b, c]
+    n_z = [send(square, square, along_z(d)) for d in (2, 1, 7)]
     z_copies = [send(mine, mine, along_z(d)) for d in (2, 1, 7)]
     basis = dot(raw_rows.astype(f32), lower, 1, 1, precise)[:OWN]
     p_all[c] = basis.astype(bf16)
@@ -367,7 +377,7 @@
 
     up_a, down_a = first_axis(1), first_axis(3)
     up_b, down_b = second_axis(1), second_axis(3)
-    a_below, a_above = lax.rem(a + 3, 4), lax.rem(a + 1, 4)
+    a_below, a_above, a_far = lax.rem(a + 3, 4), lax.rem(a + 1, 4), lax.rem(a + 2, 4)
     b_below, b_above, b_far = lax.rem(b + 3, 4), lax.rem(b + 1, 4), lax.rem(b + 2, 4)
 
     def ring_a(at):
@@ -391,11 +401,47 @@
         part = f_all.at[k, :, at]
         return send(part, part, other_core)
 
+    def finish(half, at):
+        @pl.loop(0, 2)
+        def _(pair):
+            pieces = (pair * 2, pair * 2 + 1)
+            every = [f_all[half, i, at].reshape(4 * RANK, 128) for i in pieces]
+            mean = dot(p_scaled[...], jnp.concatenate(every, axis=1), 1, 0)
+            own = [f_all[half, i, at, c] for i in pieces]
+            decay = dot(p_own[...], jnp.concatenate(own, axis=1), 1, 0)
+            for n, i in enumerate(pieces):
+                lanes = slice(n * 128, n * 128 + 128)
+                columns = pl.ds(
+                    pl.multiple_of(half * (COLS // 2) + i * 512 + at * 128, 128), 128
+                )
+                matrix = grads_v[:, columns].astype(f32) + buffer_v[:, columns].astype(f32)
+                buffer_new[:, columns] = (matrix + decay[:, lanes]).astype(bf16)
+                means[...] = mean[:, lanes]
+                carried = jnp.concatenate(
+                    [mom_all[m, :, columns].astype(f32) for m in range(4)], axis=0
+                )
+                part = mean[:, lanes]
+                anchor_new[:, columns] = (
+                    anchor_v[:, columns].astype(f32)
+                    - outer_rate * (part + outer_beta * (outer_beta * carried + part))
+                ).astype(bf16)
+                rows = pl.ds(pl.multiple_of(c * QUARTER, 8), QUARTER)
+                momentum_new[:, columns] = outer_beta * mom_v[:, columns] + means[rows, :]
+
+    for copy in n_z:
+        copy.wait_recv()
+    n_second = [send(nb.at[b], nb.at[b], second_axis(d)) for d in (2, 1, 3)]
     for copy in z_copies:
         copy.wait_recv()
     piece = f_all.at[k, a, b]
     up, down = send(piece, piece, up_b), send(piece, piece, down_b)
     ring_own = ring_a(b)
+    line_receive(2)
+    line_send(3)
+    for copy in n_second:
+        copy.wait_recv()
+    na[a] = (nb[0] + nb[1]) + (nb[2] + nb[3])
+    n_first = [send(na.at[a], na.at[a], first_axis(d)) for d in (2, 1, 3)]
     up.wait_recv()
     came = f_all.at[k, a, b_below, 0:2]
     on_up = send(came, came, up_b)
@@ -408,56 +454,67 @@
     on_up.wait_recv()
     on_down.wait_recv()
     ring_far = ring_a(b_far)
+    for copy in n_first:
+        copy.wait_recv()
+    nk[k] = (na[0] + na[1]) + (na[2] + na[3])
+    n_cross = send(nk.at[k], nk.at[k], other_core)
     below_on = forward_a(ring_below)
     above_on = forward_a(ring_above)
     crossing = [cross(own_on)]
     far_on = forward_a(ring_far)
     crossing.append(cross(below_on))
     crossing.append(cross(above_on))
-    line_receive(3)
-    crossing.append(cross(far_on))
-    for copy in crossing:
-        copy.wait_recv()
-
-    squares[...] = jnp.zeros_like(squares)
-
-    @pl.loop(0, 8)
-    def _(i):
-        for j in range(4):
-            for island in range(4):
-                values = f_all[i // 4, lax.rem(i, 4), j, island].astype(f32)
-                squares[island] += values * values
-
-    ones = jnp.ones((8, RANK), f32)
+    n_cross.wait_recv()
     for copy in p_copies:
         copy.wait_recv()
     rate = math.sqrt(ROWS * COLS / RANK) / 4.0
     for island in range(4):
-        total = dot(ones, squares[island], 1, 1, precise)[:1]
+        total = (nk[0, island] + nk[1, island])[:1]
         scale = rate * lax.rsqrt(total + epsilon)
         p_scaled[:, island * RANK : (island + 1) * RANK] = (
             p_all[island].astype(f32) * scale
         ).astype(bf16)
+    loads[3].wait()
+    line_receive(3)
+    finish(k, b)
+    finish(k, b_below)
+    finish(k, b_above)
+    crossing.append(cross(far_on))
+    for copy, at in zip(crossing, (a, a_below, a_above)):
+        copy.wait_recv()
+        finish(1 - k, at)
+    finish(k, b_far)
+    crossing[3].wait_recv()
+    finish(1 - k, a_far)
     for copy in started:
         copy.wait_send()
 
 
-def exchange(grads, buffer, q_old, momentum):
+def exchange(grads, buffer, q_old, anchor, momentum):
     vmem = pltpu.VMEM
     whole = pl.BlockSpec(memory_space=pltpu.VMEM)
-    anywhere = pl.BlockSpec(memory_space=pl.ANY)
+    anywhere = pl.BlockSpec(memory_space=pltpu.HBM)
     block = (128, 128)
     return pl.pallas_call(
         exchange_kernel,
         out_shape=(
-            jax.ShapeDtypeStruct((2, 4, 4, 4, 128, 128), bf16),
-            jax.ShapeDtypeStruct((OWN, 4 * RANK), bf16),
-            jax.ShapeDtypeStruct((OWN, RANK), bf16),
-            jax.ShapeDtypeStruct((4, QUARTER_PADDED, COLS), bf16),
+            vmem((OWN, COLS), bf16),
+            vmem((OWN, COLS), bf16),
+            vmem((QUARTER, COLS), f32),
         ),
-        in_specs=[anywhere, anywhere, whole, anywhere],
-        out_specs=(whole, whole, whole, whole),
+        in_specs=[anywhere] * 5,
+        out_specs=(whole, whole, whole),
         scratch_shapes=[
+            vmem((2, 4, 4, 4, *block), bf16),
+            vmem((OWN, 4 * RANK), bf16),
+            vmem((OWN, RANK), bf16),
+            vmem((4, QUARTER, COLS), bf16),
+            vmem((OWN, COLS), bf16),
+            vmem((OWN, 128), f32),
+            vmem((4, 4, 8, 128), f32),
+            vmem((4, 4, 8, 128), f32),
+            vmem((2, 4, 8, 128), f32),
+            vmem((64, RANK), f32),
             vmem((OWN, COLS), bf16),
             vmem((OWN, COLS), bf16),
             vmem((QUARTER, COLS), f32),
@@ -481,75 +538,20 @@
             vmem(block, bf16),
             vmem(block, bf16),
             vmem((4, OWN, RANK), bf16),
-            vmem((4, *block), f32),
-            pltpu.SemaphoreType.DMA((3,)),
-            pltpu.SemaphoreType.DMA((80,)),
-            pltpu.SemaphoreType.DMA((80,)),
+            pltpu.SemaphoreType.DMA((5,)),
+            pltpu.SemaphoreType.DMA((96,)),
+            pltpu.SemaphoreType.DMA((96,)),
         ],
-        compiler_params=pltpu.CompilerParams(collective_id=0, has_side_effects=True),
+        compiler_params=pltpu.CompilerParams(
+            collective_id=0, has_side_effects=True, vmem_limit_bytes=36 * 1024 * 1024
+        ),
         name="exchange",
-    )(grads, buffer, q_old, momentum)
-
-
-def update_kernel(
-    factors, p_scaled, p_own, mom_all, grads, buffer, anchor, momentum, anchor_new, buffer_new, momentum_new, means
-):
-    c = lax.axis_index("island")
-    pieces = STEP_COLS // 128
-    for pair in range(0, pieces, 2):
-        at = slice(pair * 128, pair * 128 + 256)
-        both = jnp.concatenate(
-            [factors[pair + i].reshape(4 * RANK, 128) for i in (0, 1)], axis=1
-        )
-        means[:, at] = dot(p_scaled[...], both, 1, 0)
-        own = jnp.concatenate([factors[pair + i, c] for i in (0, 1)], axis=1)
-        matrix = grads[:, at].astype(f32) + buffer[:, at].astype(f32)
-        buffer_new[:, at] = (matrix + dot(p_own[...], own, 1, 0)).astype(bf16)
-    carried = jnp.concatenate(
-        [mom_all[i].astype(f32)[:QUARTER] for i in range(4)], axis=0
-    )
-    mean = means[...]
-    anchor_new[...] = (
-        anchor[...].astype(f32)
-        - outer_rate * (mean + outer_beta * (outer_beta * carried + mean))
-    ).astype(bf16)
-    rows = pl.ds(pl.multiple_of(c * QUARTER, 8), QUARTER)
-    momentum_new[...] = outer_beta * momentum[...] + means[rows, :]
-
-
-def update(factors, p_scaled, p_own, mom_all, grads, buffer, anchor, momentum):
-    wide = pl.BlockSpec((OWN, STEP_COLS), lambda i: (0, i))
-    narrow = pl.BlockSpec((QUARTER, STEP_COLS), lambda i: (0, i))
-    return pl.pallas_call(
-        update_kernel,
-        grid=(COLS // STEP_COLS,),
-        out_shape=(
-            jax.ShapeDtypeStruct((OWN, COLS), bf16),
-            jax.ShapeDtypeStruct((OWN, COLS), bf16),
-            jax.ShapeDtypeStruct((QUARTER, COLS), f32),
-        ),
-        in_specs=[
-            pl.BlockSpec((STEP_COLS // 128, 4, 128, 128), lambda i: (i, 0, 0, 0)),
-            pl.BlockSpec((OWN, 4 * RANK), lambda i: (0, 0)),
-            pl.BlockSpec((OWN, RANK), lambda i: (0, 0)),
-            pl.BlockSpec((4, QUARTER_PADDED, STEP_COLS), lambda i: (0, 0, i)),
-            wide,
-            wide,
-            wide,
-            narrow,
-        ],
-        out_specs=(wide, wide, narrow),
-        scratch_shapes=[pltpu.VMEM((OWN, STEP_COLS), f32)],
-        name="update",
-    )(factors, p_scaled, p_own, mom_all, grads, buffer, anchor, momentum)
+    )(*(pltpu.with_memory_space_constraint(v, pltpu.HBM) for v in (grads, buffer, q_old, anchor, momentum)))
 
 
 def body(grads, buffer, q_old, anchor, momentum):
-    grads, buffer = grads[0, 0], buffer[0]
-    f_all, p_scaled, p_own, mom_all = exchange(grads, buffer, q_old[0], momentum)
-    factors = f_all.reshape(COLS // 128, 4, 128, 128)
-    anchor_new, buffer_new, momentum_new = update(
-        factors, p_scaled, p_own, mom_all, grads, buffer, anchor, momentum
+    anchor_new, buffer_new, momentum_new = exchange(
+        grads[0, 0], buffer[0], q_old[0], anchor, momentum
     )
     return (anchor_new, buffer_new[None], momentum_new)
 

time: 97.5 us -> 79.5 us (0.82)
  Pallas kernels: 96.6 us -> 75.4 us
  local copies, waits for them, and re-layouts: 0 us -> 3.38 us
    pallas_call x2 -> x1, Pallas kernels: 96.6 us -> 75.4 us  [exchange(): pl.pallas_call(exchange_kernel, out_shape=(vmem((OWN, COLS), bf16), vmem(...]
    unnamed x0 -> x3, local copies, waits for them, and re-layouts: none -> 3.38 us
where the time goes in v2:
time: 79.5 us; the launch traced here: 79.4 us
  Pallas kernels  75.4 us (95%)
  local copies, waits for them, and re-layouts  3.38 us (4%)
    pallas_call x1, Pallas kernels, exchange(): pl.pallas_call(exchange_kernel, out_shape=(vmem((OWN, COLS), bf16), vmem(...  75.4 us
    unnamed x3, local copies, waits for them, and re-layouts  3.38 us

profile of v2, /device:TPU:1, one launch (start us, length us, event | category | flops | bytes accessed | tf_op | source)
XLA Modules:
  0.0 79.4 jit_solution(7289323701972874322)
XLA Ops:
  0.6 75.4 %exchange.1 = (bf16[224,4096]{1,0:T(8,128)(2,1)S(1)}, bf16[224,4096]{1,0:T(8,128)(2,1)S(1)}, f32[56,4096]{1,0:T(8,128)S(1)}) custom-call(bf16[224,4096]{1,0:T(8,128)(2,1)} %bitcast.5, bf16[224,4096]{1,0:T(8,128)(2,1)} %bitcast.6, f32[64,128]{1,0:T(8,128)} %bitcast.7, bf16[224,4096]{1,0:T(8,128)(2,1)} %anchor.1, f32[56,4096]{1,0:T(8,128)} %momentum.1), custom_call_target="tpu_custom_call" | custom-call | tf_op jit(solution)/shard_map/exchange/pallas_call | solution.py:498
  76.0 1.2 %copy.11 = bf16[224,4096]{1,0:T(8,128)(2,1)} copy(bf16[224,4096]{1,0:T(8,128)(2,1)S(1)} %get-tuple-element.9) | data formatting | bytes 3670016
  77.3 1.2 %copy.12 = bf16[1,224,4096]{2,1,0:T(8,128)(2,1)} copy(bf16[1,224,4096]{2,1,0:T(8,128)(2,1)S(1)} %bitcast.4) | data formatting | bytes 3670016
  78.5 0.9 %copy.13 = f32[56,4096]{1,0:T(8,128)} copy(f32[56,4096]{1,0:T(8,128)S(1)} %get-tuple-element.11) | data formatting | bytes 1835008

commit v3 on v2

--- a/solution.py
+++ b/solution.py
@@ -90,6 +90,7 @@
     buffer_v,
     mom_v,
     mb,
+    mp,
     qa,
     raw_b,
     gsend,
@@ -139,7 +140,6 @@
     for d in (1, 2, 3):
         peers.append({"fsdp_1": lax.rem(x + d, 4)})
         peers.append({"fsdp_2": lax.rem(y + d, 4)})
-        peers.append({"fsdp_0": 1 - h, "fsdp_1": lax.rem(x + d, 4)})
         peers.append({"island": lax.rem(c + d, 4)})
     for d in (1, 2, 6, 7):
         peers.append(along_z(d))
@@ -180,33 +180,26 @@
     for at in (4, 0, 1, 2, 3):
         loads[at].start()
     loads[4].wait()
-    qa[h, x, y, k] = q_v[...].astype(bf16)
-    loads[0].wait()
-    mom_all[c] = mom_v[...].astype(bf16)
+    qa[h, k, a, b] = q_v[...].astype(bf16)
     pl.semaphore_wait(barrier, len(peers))
 
-    own_piece = qa.at[h, x, y, k]
-    q_copies = {}
-    for dh in (0, 1):
-        for dx in (1, 2, 3) if dh == 0 else (0, 1, 2, 3):
-            q_copies[dh, dx] = send(
-                own_piece,
-                own_piece,
-                {"fsdp_0": lax.rem(h + dh, 2), "fsdp_1": lax.rem(x + dx, 4)},
-            )
+    own_piece = qa.at[h, k, a, b]
+    far_piece = qa.at[1 - h, k, a, b]
+    q_far = send(own_piece, own_piece, other_half)
+    q_first = [send(own_piece, own_piece, first_axis(d)) for d in (2, 1, 3)]
 
     line = []
-    for step in (1, 2, 3):
+    for step, first, rows in ((1, 0, 56), (2, 0, 56), (3, 0, 32), (3, 32, 24)):
         up_ok = jnp.logical_and(c < 3, c >= step - 1)
         down_ok = jnp.logical_and(c > 0, c + step - 1 <= 3)
-        up_at = lax.rem(c - (step - 1) + 4, 4)
-        down_at = lax.rem(c + (step - 1), 4)
-        up = copy_to(mom_all.at[up_at], mom_all.at[up_at], {"island": lax.rem(c + 1, 4)})
-        down = copy_to(mom_all.at[down_at], mom_all.at[down_at], {"island": lax.rem(c + 3, 4)})
+        up_part = mom_all.at[lax.rem(c - (step - 1) + 4, 4), pl.ds(first, rows)]
+        down_part = mom_all.at[lax.rem(c + (step - 1), 4), pl.ds(first, rows)]
+        up = copy_to(up_part, up_part, {"island": lax.rem(c + 1, 4)})
+        down = copy_to(down_part, down_part, {"island": lax.rem(c + 3, 4)})
         line.append((up_ok, up, c - step >= 0, down_ok, down, c + step <= 3))
 
-    def line_send(step):
-        up_ok, up, _, down_ok, down, _ = line[step - 1]
+    def line_send(hop):
+        up_ok, up, _, down_ok, down, _ = line[hop]
 
         @pl.when(up_ok)
         def _():
@@ -216,8 +209,8 @@
         def _():
             down.start()
 
-    def line_receive(step):
-        up_ok, up, from_below, down_ok, down, from_above = line[step - 1]
+    def line_receive(hop):
+        up_ok, up, from_below, down_ok, down, from_above = line[hop]
 
         @pl.when(from_below)
         def _():
@@ -235,51 +228,67 @@
         def _():
             down.wait_send()
 
-    line_send(1)
+    loads[0].wait()
+    mom_all[c] = mom_v[...].astype(bf16)
+    line_send(0)
 
     loads[1].wait()
     loads[2].wait()
+
+    low_lanes = lax.broadcasted_iota(jnp.int32, (16, 128), 1) < 64
 
     @pl.loop(0, OWN // 16)
     def _(i):
         at = pl.ds(pl.multiple_of(i * 16, 16), 16)
-        mb[at, :] = (grads_v[at, :].astype(f32) + buffer_v[at, :].astype(f32)).astype(bf16)
+        matrix = grads_v[at, :].astype(f32) + buffer_v[at, :].astype(f32)
+        mb[at, :] = matrix.astype(bf16)
+
+        def block(half, row, column):
+            first = (half * 16 + row * 4 + column) * 128
+            return matrix[:, first : first + 128]
+
+        for half in (0, 1):
+            for outer in range(4):
+                for pair in (0, 1):
+                    lanes = slice((outer * 2 + pair) * 128, (outer * 2 + pair + 1) * 128)
+                    one, two = block(half, outer, pair * 2), block(half, outer, pair * 2 + 1)
+                    mp[half, 0, at, lanes] = jnp.where(
+                        low_lanes, one, pltpu.roll(two, 64, 1)
+                    ).astype(bf16)
+                    one, two = block(half, pair * 2, outer), block(half, pair * 2 + 1, outer)
+                    mp[half, 1, at, lanes] = jnp.where(
+                        low_lanes, pltpu.roll(one, 64, 1), two
+                    ).astype(bf16)
 
     mb[OWN:, :] = jnp.zeros((PADDED - OWN, COLS), bf16)
-
-    up_y = {"fsdp_2": lax.rem(y + 1, 4)}
-    down_y = {"fsdp_2": lax.rem(y + 3, 4)}
-    below, above = lax.rem(y + 3, 4), lax.rem(y + 1, 4)
-    q_ring = []
-    for group in (0, 1):
-        at = lax.rem(h + group, 2)
-        for dx in (1, 2, 3) if group == 0 else (0, 1, 2, 3):
-            q_copies[group, dx].wait_recv()
-        mine = qa.at[at, :, y, k]
-        q_ring.append((at, send(mine, mine, up_y), send(mine, mine, down_y)))
-    q_forward = []
-    for at, up, down in q_ring:
-        up.wait_recv()
-        came = qa.at[at, 0:2, below, k]
-        on_up = send(came, came, up_y)
-        down.wait_recv()
-        came = qa.at[at, 2:4, above, k]
-        on_down = send(came, came, down_y)
-        q_forward.append((at, on_up, on_down))
+    for half in (0, 1):
+        for core in (0, 1):
+            mp[half, core, OWN:, :] = jnp.zeros((PADDED - OWN, COLS // 4), bf16)
+
+    def gathered(at, copies):
+        for copy in copies:
+            copy.wait_recv()
+        mine = qa.at[at, k, :, b]
+        return (at, [send(mine, mine, second_axis(d)) for d in (2, 1, 3)])
+
+    q_second = [gathered(h, q_first)]
+    q_far.wait_recv()
+    q_first = [send(far_piece, far_piece, first_axis(d)) for d in (2, 1, 3)]
+    q_second.append(gathered(1 - h, q_first))
     q_cross = []
-    for at, on_up, on_down in q_forward:
-        on_up.wait_recv()
-        on_down.wait_recv()
-        half = qa.at[at, :, :, k]
+    for at, copies in q_second:
+        for copy in copies:
+            copy.wait_recv()
+        half = qa.at[at, k]
         q_cross.append((at, send(half, half, other_core)))
 
-    line_receive(1)
-    line_send(2)
+    line_receive(0)
+    line_send(1)
     raw = jnp.zeros((PADDED, RANK), f32)
     for at, copy in q_cross:
-        copy.wait_recv()
-        columns = pl.ds(pl.multiple_of(at * (COLS // 2), COLS // 2), COLS // 2)
-        raw = raw + dot(mb[:, columns], qa[at].reshape(COLS // 2, RANK), 1, 0)
+        raw = raw + dot(mp[at, k], qa[at, k].reshape(COLS // 4, RANK), 1, 0)
+        copy.wait_recv()
+        raw = raw + dot(mp[at, 1 - k], qa[at, 1 - k].reshape(COLS // 4, RANK), 1, 0)
     raw_b[...] = raw.astype(bf16)
     raw_rows = raw_b[...]
 
@@ -352,6 +361,8 @@
         s2[b] + ((r3[0].astype(f32) + r3[1].astype(f32)) + r3[2].astype(f32))
     ).astype(bf16)
     r_third = send(s3b, r4, other_half)
+    line_receive(1)
+    line_send(2)
 
     gram_third.wait_recv()
     gfull[k] = g4[0] + g4[1]
@@ -362,52 +373,44 @@
     r_third.wait_recv()
     image_sum = s3b[...].astype(f32) + r4[...].astype(f32)
     factor = dot(lower, image_sum, 1, 0, precise).astype(bf16)
-    f_all[k, a, b, c] = factor
+    f_all[k, a, b, 0] = factor
     squared = jnp.square(factor.astype(f32))
     nb[b, c] = dot(jnp.ones((8, RANK), f32), squared, 1, 1, precise)
 
-    mine = f_all.at[k, a, b, c]
     square = nb.at[b, c]
     n_z = [send(square, square, along_z(d)) for d in (2, 1, 7)]
-    z_copies = [send(mine, mine, along_z(d)) for d in (2, 1, 7)]
+    z_copies = []
+    for d, rows in ((2, pl.ds(0, 64)), (6, pl.ds(64, 64)), (1, pl.ds(0, 128)), (7, pl.ds(0, 128))):
+        mine = f_all.at[k, a, b, 0, rows]
+        z_copies.append(send(mine, f_all.at[k, a, b, (-d) % 4, rows], along_z(d)))
+
+    up_a, down_a = first_axis(1), first_axis(3)
+    up_b, down_b = second_axis(1), second_axis(3)
+    a_below, a_above, a_far = lax.rem(a + 3, 4), lax.rem(a + 1, 4), lax.rem(a + 2, 4)
+    b_below, b_above, b_far = lax.rem(b + 3, 4), lax.rem(b + 1, 4), lax.rem(b + 2, 4)
+
+    def pass_on(at, islands, *devices):
+        part = f_all.at[k, at[0], at[1], pl.ds(islands[0], islands[1] - islands[0])]
+        return [send(part, part, device) for device in devices]
+
+    early_b = pass_on((a, b), (0, 1), up_b, down_b)
+    early_a = pass_on((a, b), (0, 1), up_a, down_a)
     basis = dot(raw_rows.astype(f32), lower, 1, 1, precise)[:OWN]
     p_all[c] = basis.astype(bf16)
     p_copies = [send(p_all.at[c], p_all.at[c], {"island": lax.rem(c + d, 4)}) for d in (1, 2, 3)]
     p_own[...] = (basis * (error_decay - 1.0)).astype(bf16)
 
-    up_a, down_a = first_axis(1), first_axis(3)
-    up_b, down_b = second_axis(1), second_axis(3)
-    a_below, a_above, a_far = lax.rem(a + 3, 4), lax.rem(a + 1, 4), lax.rem(a + 2, 4)
-    b_below, b_above, b_far = lax.rem(b + 3, 4), lax.rem(b + 1, 4), lax.rem(b + 2, 4)
-
-    def ring_a(at):
-        piece = f_all.at[k, a, at]
-        return (at, send(piece, piece, up_a), send(piece, piece, down_a))
-
-    def forward_a(ring):
-        at, up, down = ring
-        up.wait_recv()
-        came = f_all.at[k, a_below, at, 0:2]
-        on_up = send(came, came, up_a)
-        down.wait_recv()
-        came = f_all.at[k, a_above, at, 2:4]
-        on_down = send(came, came, down_a)
-        return (at, on_up, on_down)
-
-    def cross(ring):
-        at, on_up, on_down = ring
-        on_up.wait_recv()
-        on_down.wait_recv()
-        part = f_all.at[k, :, at]
-        return send(part, part, other_core)
+    order = [lax.rem(m - c + 4, 4) for m in range(4)]
 
     def finish(half, at):
-        @pl.loop(0, 2)
-        def _(pair):
+        for pair in (0, 1):
             pieces = (pair * 2, pair * 2 + 1)
-            every = [f_all[half, i, at].reshape(4 * RANK, 128) for i in pieces]
+            every = [
+                jnp.concatenate([f_all[half, i, at, order[m]] for m in range(4)], axis=0)
+                for i in pieces
+            ]
             mean = dot(p_scaled[...], jnp.concatenate(every, axis=1), 1, 0)
-            own = [f_all[half, i, at, c] for i in pieces]
+            own = [f_all[half, i, at, 0] for i in pieces]
             decay = dot(p_own[...], jnp.concatenate(own, axis=1), 1, 0)
             for n, i in enumerate(pieces):
                 lanes = slice(n * 128, n * 128 + 128)
@@ -428,42 +431,62 @@
                 rows = pl.ds(pl.multiple_of(c * QUARTER, 8), QUARTER)
                 momentum_new[:, columns] = outer_beta * mom_v[:, columns] + means[rows, :]
 
+    for copy in early_b:
+        copy.wait_recv()
+    early_b_on = pass_on((a, b_above), (0, 1), down_b)
+    early_below = pass_on((a, b_below), (0, 1), up_a, down_a)
+    early_above = pass_on((a, b_above), (0, 1), up_a, down_a)
+    for copy in early_a:
+        copy.wait_recv()
+    early_a_on = pass_on((a_above, b), (0, 1), down_a)
+
     for copy in n_z:
         copy.wait_recv()
     n_second = [send(nb.at[b], nb.at[b], second_axis(d)) for d in (2, 1, 3)]
     for copy in z_copies:
         copy.wait_recv()
-    piece = f_all.at[k, a, b]
-    up, down = send(piece, piece, up_b), send(piece, piece, down_b)
-    ring_own = ring_a(b)
-    line_receive(2)
+    up_copy, down_copy = pass_on((a, b), (1, 4), up_b, down_b)
+    own_up, own_down = pass_on((a, b), (1, 4), up_a, down_a)
     line_send(3)
     for copy in n_second:
         copy.wait_recv()
     na[a] = (nb[0] + nb[1]) + (nb[2] + nb[3])
     n_first = [send(na.at[a], na.at[a], first_axis(d)) for d in (2, 1, 3)]
-    up.wait_recv()
-    came = f_all.at[k, a, b_below, 0:2]
-    on_up = send(came, came, up_b)
-    down.wait_recv()
-    came = f_all.at[k, a, b_above, 2:4]
-    on_down = send(came, came, down_b)
-    ring_below = ring_a(b_below)
-    ring_above = ring_a(b_above)
-    own_on = forward_a(ring_own)
-    on_up.wait_recv()
-    on_down.wait_recv()
-    ring_far = ring_a(b_far)
+    up_copy.wait_recv()
+    b_on = pass_on((a, b_below), (2, 4), up_b)
+    down_copy.wait_recv()
+    b_on += pass_on((a, b_above), (1, 2), down_b)
+    below_up, below_down = pass_on((a, b_below), (1, 4), up_a, down_a)
+    above_up, above_down = pass_on((a, b_above), (1, 4), up_a, down_a)
+    own_up.wait_recv()
+    own_on = pass_on((a_below, b), (2, 4), up_a)
+    own_down.wait_recv()
+    own_on += pass_on((a_above, b), (1, 2), down_a)
+    for copy in early_b_on + b_on:
+        copy.wait_recv()
+    far_up, far_down = pass_on((a, b_far), (0, 4), up_a, down_a)
     for copy in n_first:
         copy.wait_recv()
     nk[k] = (na[0] + na[1]) + (na[2] + na[3])
     n_cross = send(nk.at[k], nk.at[k], other_core)
-    below_on = forward_a(ring_below)
-    above_on = forward_a(ring_above)
-    crossing = [cross(own_on)]
-    far_on = forward_a(ring_far)
-    crossing.append(cross(below_on))
-    crossing.append(cross(above_on))
+
+    def forward_a(at, early, up, down):
+        for copy in early:
+            copy.wait_recv()
+        up.wait_recv()
+        on = pass_on((a_below, at), (2, 4), up_a)
+        down.wait_recv()
+        return on + pass_on((a_above, at), (0, 2), down_a)
+
+    def cross(at, arriving):
+        for copy in arriving:
+            copy.wait_recv()
+        part = f_all.at[k, :, at]
+        return send(part, part, other_core)
+
+    below_on = forward_a(b_below, early_below, below_up, below_down)
+    above_on = forward_a(b_above, early_above, above_up, above_down)
+    crossing = [cross(b, early_a_on + own_on)]
     n_cross.wait_recv()
     for copy in p_copies:
         copy.wait_recv()
@@ -475,14 +498,20 @@
             p_all[island].astype(f32) * scale
         ).astype(bf16)
     loads[3].wait()
+    far_on = forward_a(b_far, [], far_up, far_down)
+    line_receive(2)
     line_receive(3)
     finish(k, b)
+    crossing.append(cross(b_below, below_on))
+    crossing.append(cross(b_above, above_on))
+    crossing[0].wait_recv()
+    finish(1 - k, a)
     finish(k, b_below)
+    crossing.append(cross(b_far, far_on))
+    for copy, at in zip(crossing[1:3], (a_below, a_above)):
+        copy.wait_recv()
+        finish(1 - k, at)
     finish(k, b_above)
-    crossing.append(cross(far_on))
-    for copy, at in zip(crossing, (a, a_below, a_above)):
-        copy.wait_recv()
-        finish(1 - k, at)
     finish(k, b_far)
     crossing[3].wait_recv()
     finish(1 - k, a_far)
@@ -519,7 +548,8 @@
             vmem((OWN, COLS), bf16),
             vmem((QUARTER, COLS), f32),
             vmem((PADDED, COLS), bf16),
-            vmem((2, 4, 4, 2, 64, RANK), bf16),
+            vmem((2, 2, PADDED, COLS // 4), bf16),
+            vmem((2, 2, 4, 4, 64, RANK), bf16),
             vmem((PADDED, RANK), bf16),
             vmem((2, 64, 128), f32),
             vmem((64, 128), f32),
@@ -539,8 +569,8 @@
             vmem(block, bf16),
             vmem((4, OWN, RANK), bf16),
             pltpu.SemaphoreType.DMA((5,)),
-            pltpu.SemaphoreType.DMA((96,)),
-            pltpu.SemaphoreType.DMA((96,)),
+            pltpu.SemaphoreType.DMA((128,)),
+            pltpu.SemaphoreType.DMA((128,)),
         ],
         compiler_params=pltpu.CompilerParams(
             collective_id=0, has_side_effects=True, vmem_limit_bytes=36 * 1024 * 1024
@@ -549,9 +579,42 @@
     )(*(pltpu.with_memory_space_constraint(v, pltpu.HBM) for v in (grads, buffer, q_old, anchor, momentum)))
 
 
+def store_kernel(anchor_v, buffer_v, momentum_v, anchor_new, buffer_new, momentum_new, sems):
+    copies = []
+    for source, target, parts in (
+        (anchor_v, anchor_new, 4),
+        (buffer_v, buffer_new, 4),
+        (momentum_v, momentum_new, 1),
+    ):
+        height = source.shape[0] // parts
+        for part in range(parts):
+            rows = pl.ds(part * height, height)
+            copy = pltpu.make_async_copy(source.at[rows], target.at[rows], sems.at[len(copies)])
+            copy.start()
+            copies.append(copy)
+    for copy in copies:
+        copy.wait()
+
+
+def store(anchor_new, buffer_new, momentum_new):
+    return pl.pallas_call(
+        store_kernel,
+        out_shape=(
+            jax.ShapeDtypeStruct((OWN, COLS), bf16),
+            jax.ShapeDtypeStruct((OWN, COLS), bf16),
+            jax.ShapeDtypeStruct((QUARTER, COLS), f32),
+        ),
+        in_specs=[pl.BlockSpec(memory_space=pltpu.VMEM)] * 3,
+        out_specs=[pl.BlockSpec(memory_space=pltpu.HBM)] * 3,
+        scratch_shapes=[pltpu.SemaphoreType.DMA((9,))],
+        compiler_params=pltpu.CompilerParams(vmem_limit_bytes=1024 * 1024),
+        name="store",
+    )(anchor_new, buffer_new, momentum_new)
+
+
 def body(grads, buffer, q_old, anchor, momentum):
-    anchor_new, buffer_new, momentum_new = exchange(
-        grads[0, 0], buffer[0], q_old[0], anchor, momentum
+    anchor_new, buffer_new, momentum_new = store(
+        *exchange(grads[0, 0], buffer[0], q_old[0], anchor, momentum)
     )
     return (anchor_new, buffer_new[None], momentum_new)
 

time: 79.5 us -> 72.8 us (0.916)
  local copies, waits for them, and re-layouts: 3.38 us -> 0 us
  Pallas kernels: 75.4 us -> 72.1 us
    pallas_call x1, Pallas kernels: 75.4 us -> 69.8 us  [exchange(): pl.pallas_call(exchange_kernel, out_shape=(vmem((OWN, COLS), bf16), vmem(...]
    unnamed x3 -> x0, local copies, waits for them, and re-layouts: 3.38 us -> none
    pallas_call x0 -> x1, Pallas kernels: none -> 2.21 us  [store(): pl.pallas_call(store_kernel, out_shape=(jax.ShapeDtypeStruct((OWN, COLS),...]
where the time goes in v3:
time: 72.8 us; the launch traced here: 72.7 us
  Pallas kernels  72.1 us (99%)
    pallas_call x1, Pallas kernels, exchange(): pl.pallas_call(exchange_kernel, out_shape=(vmem((OWN, COLS), bf16), vmem(...  69.8 us
    pallas_call x1, Pallas kernels, store(): pl.pallas_call(store_kernel, out_shape=(jax.ShapeDtypeStruct((OWN, COLS),...  2.21 us

profile of v3, /device:TPU:1, one launch (start us, length us, event | category | flops | bytes accessed | tf_op | source)
XLA Modules:
  0.0 72.7 jit_solution(14223615063959191223)
XLA Ops:
  0.6 69.8 %exchange.1 = (bf16[224,4096]{1,0:T(8,128)(2,1)S(1)}, bf16[224,4096]{1,0:T(8,128)(2,1)S(1)}, f32[56,4096]{1,0:T(8,128)S(1)}) custom-call(bf16[224,4096]{1,0:T(8,128)(2,1)} %bitcast.4, bf16[224,4096]{1,0:T(8,128)(2,1)} %bitcast.5, f32[64,128]{1,0:T(8,128)} %bitcast.6, bf16[224,4096]{1,0:T(8,128)(2,1)} %anchor.1, f32[56,4096]{1,0:T(8,128)} %momentum.1), custom_call_target="tpu_custom_call" | custom-call | tf_op jit(solution)/shard_map/exchange/pallas_call | solution.py:527
  70.5 2.2 %store.1 = (bf16[224,4096]{1,0:T(8,128)(2,1)}, bf16[224,4096]{1,0:T(8,128)(2,1)}, f32[56,4096]{1,0:T(8,128)}) custom-call(bf16[224,4096]{1,0:T(8,128)(2,1)S(1)} %get-tuple-element.9.anchor_v, bf16[224,4096]{1,0:T(8,128)(2,1)S(1)} %get-tuple-element.10.buffer_v, f32[56,4096]{1,0:T(8,128)S(1)} %get-tuple-element.11.momentum_v), custom_call_target="tpu_custom_call" | custom-call | tf_op jit(solution)/shard_map/store/pallas_call | solution.py:600

commit v4 on v3

--- a/solution.py
+++ b/solution.py
@@ -183,13 +183,20 @@
     qa[h, k, a, b] = q_v[...].astype(bf16)
     pl.semaphore_wait(barrier, len(peers))
 
+    def along_second(part):
+        return [send(part, part, second_axis(d)) for d in (2, 1, 3)]
+
+    def first_sends(part):
+        return {d: send(part, part, first_axis(d)) for d in (2, 1, 3)}
+
     own_piece = qa.at[h, k, a, b]
     far_piece = qa.at[1 - h, k, a, b]
     q_far = send(own_piece, own_piece, other_half)
-    q_first = [send(own_piece, own_piece, first_axis(d)) for d in (2, 1, 3)]
+    q_first = first_sends(own_piece)
+    on_near = along_second(own_piece)
 
     line = []
-    for step, first, rows in ((1, 0, 56), (2, 0, 56), (3, 0, 32), (3, 32, 24)):
+    for step, first, rows in ((1, 0, 56), (2, 0, 40), (2, 40, 16), (3, 0, 24), (3, 24, 32)):
         up_ok = jnp.logical_and(c < 3, c >= step - 1)
         down_ok = jnp.logical_and(c > 0, c + step - 1 <= 3)
         up_part = mom_all.at[lax.rem(c - (step - 1) + 4, 4), pl.ds(first, rows)]
@@ -265,16 +272,19 @@
         for core in (0, 1):
             mp[half, core, OWN:, :] = jnp.zeros((PADDED - OWN, COLS // 4), bf16)
 
-    def gathered(at, copies):
-        for copy in copies:
-            copy.wait_recv()
-        mine = qa.at[at, k, :, b]
-        return (at, [send(mine, mine, second_axis(d)) for d in (2, 1, 3)])
-
-    q_second = [gathered(h, q_first)]
+    def arrived(at, copies):
+        on = []
+        for d in (1, 3, 2):
+            copies[d].wait_recv()
+            on += along_second(qa.at[at, k, lax.rem(a + 4 - d, 4), b])
+        return on
+
+    on_near += arrived(h, q_first)
     q_far.wait_recv()
-    q_first = [send(far_piece, far_piece, first_axis(d)) for d in (2, 1, 3)]
-    q_second.append(gathered(1 - h, q_first))
+    q_first = first_sends(far_piece)
+    on_far = along_second(far_piece)
+    on_far += arrived(1 - h, q_first)
+    q_second = [(h, on_near), (1 - h, on_far)]
     q_cross = []
     for at, copies in q_second:
         for copy in copies:
@@ -292,6 +302,10 @@
     raw_b[...] = raw.astype(bf16)
     raw_rows = raw_b[...]
 
+    def total_of(parts):
+        one, two, three, four = (parts[i].astype(f32) for i in range(4))
+        return (one + two) + (three + four)
+
     gram = dot(raw_rows, raw_rows, 0, 0)
     gsend[0] = gram[:64]
     gsend[1] = gram[64:]
@@ -318,12 +332,12 @@
         piece = pl.ds(chunk * 8, 8)
         r_cross.append(send(rp.at[piece], r1.at[piece], other_core))
 
-    gram_cross.wait_recv()
-    g2[a] = gsend[k] + g1[...]
-    gram_first = [send(g2.at[a], g2.at[a], first_axis(d)) for d in (2, 1, 3)]
-
     for part in range(8):
         image(k, part, store_near)
+
+    gram_cross.wait_recv()
+    g2[a] = (gsend[k] + g1[...]).astype(bf16)
+    gram_first = [send(g2.at[a], g2.at[a], first_axis(d)) for d in (2, 1, 3)]
 
     for copy in r_cross:
         copy.wait_recv()
@@ -336,7 +350,7 @@
 
     for copy in gram_first:
         copy.wait_recv()
-    g3[b] = (g2[0] + g2[1]) + (g2[2] + g2[3])
+    g3[b] = total_of(g2).astype(bf16)
     gram_second = [send(g3.at[b], g3.at[b], second_axis(d)) for d in (2, 1, 3)]
 
     for copy in r_first:
@@ -352,7 +366,7 @@
 
     for copy in gram_second:
         copy.wait_recv()
-    g4[h] = (g3[0] + g3[1]) + (g3[2] + g3[3])
+    g4[h] = total_of(g3).astype(bf16)
     gram_third = send(g4.at[h], g4.at[h], other_half)
 
     for copy in r_second:
@@ -363,9 +377,10 @@
     r_third = send(s3b, r4, other_half)
     line_receive(1)
     line_send(2)
+    line_send(3)
 
     gram_third.wait_recv()
-    gfull[k] = g4[0] + g4[1]
+    gfull[k] = g4[0].astype(f32) + g4[1].astype(f32)
     gram_last = send(gfull.at[k], gfull.at[k], other_core)
     gram_last.wait_recv()
     lower = inverse_lower(jnp.concatenate([gfull[0], gfull[1]], axis=0))
@@ -402,9 +417,8 @@
 
     order = [lax.rem(m - c + 4, 4) for m in range(4)]
 
-    def finish(half, at):
-        for pair in (0, 1):
-            pieces = (pair * 2, pair * 2 + 1)
+    def finish(half, at, groups=((0, 1), (2, 3))):
+        for pieces in groups:
             every = [
                 jnp.concatenate([f_all[half, i, at, order[m]] for m in range(4)], axis=0)
                 for i in pieces
@@ -446,25 +460,26 @@
     for copy in z_copies:
         copy.wait_recv()
     up_copy, down_copy = pass_on((a, b), (1, 4), up_b, down_b)
-    own_up, own_down = pass_on((a, b), (1, 4), up_a, down_a)
-    line_send(3)
+    line_receive(2)
+    line_send(4)
     for copy in n_second:
         copy.wait_recv()
     na[a] = (nb[0] + nb[1]) + (nb[2] + nb[3])
     n_first = [send(na.at[a], na.at[a], first_axis(d)) for d in (2, 1, 3)]
+    own_up, own_down = pass_on((a, b), (1, 4), up_a, down_a)
     up_copy.wait_recv()
     b_on = pass_on((a, b_below), (2, 4), up_b)
     down_copy.wait_recv()
     b_on += pass_on((a, b_above), (1, 2), down_b)
     below_up, below_down = pass_on((a, b_below), (1, 4), up_a, down_a)
     above_up, above_down = pass_on((a, b_above), (1, 4), up_a, down_a)
+    for copy in early_b_on + b_on:
+        copy.wait_recv()
+    far_up, far_down = pass_on((a, b_far), (0, 4), up_a, down_a)
     own_up.wait_recv()
     own_on = pass_on((a_below, b), (2, 4), up_a)
     own_down.wait_recv()
     own_on += pass_on((a_above, b), (1, 2), down_a)
-    for copy in early_b_on + b_on:
-        copy.wait_recv()
-    far_up, far_down = pass_on((a, b_far), (0, 4), up_a, down_a)
     for copy in n_first:
         copy.wait_recv()
     nk[k] = (na[0] + na[1]) + (na[2] + na[3])
@@ -486,7 +501,13 @@
 
     below_on = forward_a(b_below, early_below, below_up, below_down)
     above_on = forward_a(b_above, early_above, above_up, above_down)
-    crossing = [cross(b, early_a_on + own_on)]
+    far_on = forward_a(b_far, [], far_up, far_down)
+    far_cross = []
+    for i in (a, a_below, a_above, a_far):
+        part = f_all.at[k, i, b_far]
+        far_cross.append(copy_to(part, part, other_core))
+    for copy in far_cross[:3]:
+        copy.start()
     n_cross.wait_recv()
     for copy in p_copies:
         copy.wait_recv()
@@ -498,23 +519,29 @@
             p_all[island].astype(f32) * scale
         ).astype(bf16)
     loads[3].wait()
-    far_on = forward_a(b_far, [], far_up, far_down)
-    line_receive(2)
+    crossing = [cross(b, early_a_on + own_on)]
     line_receive(3)
+    line_receive(4)
     finish(k, b)
     crossing.append(cross(b_below, below_on))
     crossing.append(cross(b_above, above_on))
+    finish(k, b_below)
+    finish(k, b_above)
     crossing[0].wait_recv()
     finish(1 - k, a)
-    finish(k, b_below)
-    crossing.append(cross(b_far, far_on))
+    for copy in far_on:
+        copy.wait_recv()
+    far_cross[3].start()
     for copy, at in zip(crossing[1:3], (a_below, a_above)):
         copy.wait_recv()
         finish(1 - k, at)
-    finish(k, b_above)
     finish(k, b_far)
-    crossing[3].wait_recv()
-    finish(1 - k, a_far)
+    for copy in far_cross[:3]:
+        copy.wait_recv()
+    finish(1 - k, a_far, ((b_below, b_above),))
+    far_cross[3].wait_recv()
+    finish(1 - k, a_far, ((b, b_far),))
+    started.extend(far_cross)
     for copy in started:
         copy.wait_send()
 
@@ -553,9 +580,9 @@
             vmem((PADDED, RANK), bf16),
             vmem((2, 64, 128), f32),
             vmem((64, 128), f32),
-            vmem((4, 64, 128), f32),
-            vmem((4, 64, 128), f32),
-            vmem((2, 64, 128), f32),
+            vmem((4, 64, 128), bf16),
+            vmem((4, 64, 128), bf16),
+            vmem((2, 64, 128), bf16),
             vmem((2, 64, 128), f32),
             vmem((16, *block), bf16),
             vmem((16, *block), f32),
@@ -569,8 +596,8 @@
             vmem(block, bf16),
             vmem((4, OWN, RANK), bf16),
             pltpu.SemaphoreType.DMA((5,)),
-            pltpu.SemaphoreType.DMA((128,)),
-            pltpu.SemaphoreType.DMA((128,)),
+            pltpu.SemaphoreType.DMA((160,)),
+            pltpu.SemaphoreType.DMA((160,)),
         ],
         compiler_params=pltpu.CompilerParams(
             collective_id=0, has_side_effects=True, vmem_limit_bytes=36 * 1024 * 1024
@@ -582,9 +609,9 @@
 def store_kernel(anchor_v, buffer_v, momentum_v, anchor_new, buffer_new, momentum_new, sems):
     copies = []
     for source, target, parts in (
-        (anchor_v, anchor_new, 4),
-        (buffer_v, buffer_new, 4),
-        (momentum_v, momentum_new, 1),
+        (anchor_v, anchor_new, 7),
+        (buffer_v, buffer_new, 7),
+        (momentum_v, momentum_new, 7),
     ):
         height = source.shape[0] // parts
         for part in range(parts):
@@ -606,7 +633,7 @@
         ),
         in_specs=[pl.BlockSpec(memory_space=pltpu.VMEM)] * 3,
         out_specs=[pl.BlockSpec(memory_space=pltpu.HBM)] * 3,
-        scratch_shapes=[pltpu.SemaphoreType.DMA((9,))],
+        scratch_shapes=[pltpu.SemaphoreType.DMA((21,))],
         compiler_params=pltpu.CompilerParams(vmem_limit_bytes=1024 * 1024),
         name="store",
     )(anchor_new, buffer_new, momentum_new)

time: 72.8 us -> 71.2 us (0.978)
  Pallas kernels: 72.1 us -> 70.5 us
    pallas_call x1, Pallas kernels: 69.8 us -> 68.2 us  [exchange(): pl.pallas_call(exchange_kernel, out_shape=(vmem((OWN, COLS), bf16), vmem(...]
where the time goes in v4:
time: 71.2 us; the launch traced here: 71.1 us
  Pallas kernels  70.5 us (99%)
    pallas_call x1, Pallas kernels, exchange(): pl.pallas_call(exchange_kernel, out_shape=(vmem((OWN, COLS), bf16), vmem(...  68.2 us
    pallas_call x1, Pallas kernels, store(): pl.pallas_call(store_kernel, out_shape=(jax.ShapeDtypeStruct((OWN, COLS),...  2.3 us

profile of v4, /device:TPU:1, one launch (start us, length us, event | category | flops | bytes accessed | tf_op | source)
XLA Modules:
  0.0 71.1 jit_solution(9015607361870277490)
XLA Ops:
  0.6 68.2 %exchange.1 = (bf16[224,4096]{1,0:T(8,128)(2,1)S(1)}, bf16[224,4096]{1,0:T(8,128)(2,1)S(1)}, f32[56,4096]{1,0:T(8,128)S(1)}) custom-call(bf16[224,4096]{1,0:T(8,128)(2,1)} %bitcast.4, bf16[224,4096]{1,0:T(8,128)(2,1)} %bitcast.5, f32[64,128]{1,0:T(8,128)} %bitcast.6, bf16[224,4096]{1,0:T(8,128)(2,1)} %anchor.1, f32[56,4096]{1,0:T(8,128)} %momentum.1), custom_call_target="tpu_custom_call" | custom-call | tf_op jit(solution)/shard_map/exchange/pallas_call | solution.py:554
  68.8 2.3 %store.1 = (bf16[224,4096]{1,0:T(8,128)(2,1)}, bf16[224,4096]{1,0:T(8,128)(2,1)}, f32[56,4096]{1,0:T(8,128)}) custom-call(bf16[224,4096]{1,0:T(8,128)(2,1)S(1)} %get-tuple-element.9.anchor_v, bf16[224,4096]{1,0:T(8,128)(2,1)S(1)} %get-tuple-element.10.buffer_v, f32[56,4096]{1,0:T(8,128)S(1)} %get-tuple-element.11.momentum_v), custom_call_target="tpu_custom_call" | custom-call | tf_op jit(solution)/shard_map/store/pallas_call | solution.py:627

commit v5 on v4

--- a/solution.py
+++ b/solution.py
@@ -16,6 +16,7 @@
 OWN = 224
 PADDED = 256
 QUARTER = 56
+SENDS, RECEIVES = 64, 115
 MESH = pl.DeviceIdType.MESH
 
 precise = lax.Precision.HIGHEST
@@ -67,6 +68,41 @@
     return jnp.concatenate(done, axis=0)
 
 
+def first_column(half, i, at):
+    return pl.multiple_of(half * (COLS // 2) + i * 512 + at * 128, 128)
+
+
+def finish_columns(c, half, at, held, outs, means, place=None):
+    f_all, p_scaled, p_own, mom_all, grads_v, buffer_v, anchor_v, mom_v = held
+    anchor_new, buffer_new, momentum_new = outs
+    order = [lax.rem(m - c + 4, 4) for m in range(4)]
+    for pieces in ((0, 1), (2, 3)):
+        every = [
+            jnp.concatenate([f_all[half, i, at, order[m]] for m in range(4)], axis=0)
+            for i in pieces
+        ]
+        mean = dot(p_scaled[...], jnp.concatenate(every, axis=1), 1, 0)
+        own = [f_all[half, i, at, 0] for i in pieces]
+        decay = dot(p_own[...], jnp.concatenate(own, axis=1), 1, 0)
+        for n, i in enumerate(pieces):
+            lanes = slice(n * 128, n * 128 + 128)
+            columns = pl.ds(first_column(half, i, at), 128)
+            target = columns if place is None else pl.ds((place + i) * 128, 128)
+            matrix = grads_v[:, columns].astype(f32) + buffer_v[:, columns].astype(f32)
+            buffer_new[:, target] = (matrix + decay[:, lanes]).astype(bf16)
+            part = mean[:, lanes]
+            means[...] = part
+            carried = jnp.concatenate(
+                [mom_all[m, :, columns].astype(f32) for m in range(4)], axis=0
+            )
+            anchor_new[:, target] = (
+                anchor_v[:, columns].astype(f32)
+                - outer_rate * (part + outer_beta * (outer_beta * carried + part))
+            ).astype(bf16)
+            rows = pl.ds(pl.multiple_of(c * QUARTER, 8), QUARTER)
+            momentum_new[:, target] = outer_beta * mom_v[:, columns] + means[rows, :]
+
+
 def exchange_kernel(
     grads,
     buffer,
@@ -80,15 +116,15 @@
     p_scaled,
     p_own,
     mom_all,
+    grads_v,
+    buffer_v,
     anchor_v,
+    mom_v,
     means,
     nb,
     na,
     nk,
     q_v,
-    grads_v,
-    buffer_v,
-    mom_v,
     mb,
     mp,
     qa,
@@ -144,27 +180,32 @@
     for d in (1, 2, 6, 7):
         peers.append(along_z(d))
 
-    counter = [0]
+    receives = iter(range(RECEIVES))
+    free = list(range(SENDS))
     started = []
 
-    def copy_to(src, dst, device):
-        at = counter[0]
-        counter[0] += 1
-        copy = pltpu.make_async_remote_copy(
+    def copy_to(src, dst, device, at=None):
+        return pltpu.make_async_remote_copy(
             src_ref=src,
             dst_ref=dst,
-            send_sem=send_sem.at[at],
-            recv_sem=recv_sem.at[at],
+            send_sem=send_sem.at[free.pop() if at is None else at],
+            recv_sem=recv_sem.at[next(receives)],
             device_id=device,
             device_id_type=MESH,
         )
+
+    def send(src, dst, device):
+        at = free.pop()
+        copy = copy_to(src, dst, device, at)
+        copy.start()
+        started.append((at, copy))
         return copy
 
-    def send(src, dst, device):
-        copy = copy_to(src, dst, device)
-        copy.start()
-        started.append(copy)
-        return copy
+    def sends_done():
+        for at, copy in started:
+            copy.wait_send()
+            free.append(at)
+        started.clear()
 
     barrier = pltpu.get_barrier_semaphore()
     for peer in peers:
@@ -196,7 +237,7 @@
     on_near = along_second(own_piece)
 
     line = []
-    for step, first, rows in ((1, 0, 56), (2, 0, 40), (2, 40, 16), (3, 0, 24), (3, 24, 32)):
+    for step, first, rows in ((1, 0, 56), (2, 0, 40), (2, 40, 16), (3, 0, 16), (3, 16, 40)):
         up_ok = jnp.logical_and(c < 3, c >= step - 1)
         down_ok = jnp.logical_and(c > 0, c + step - 1 <= 3)
         up_part = mom_all.at[lax.rem(c - (step - 1) + 4, 4), pl.ds(first, rows)]
@@ -306,6 +347,7 @@
         one, two, three, four = (parts[i].astype(f32) for i in range(4))
         return (one + two) + (three + four)
 
+    sends_done()
     gram = dot(raw_rows, raw_rows, 0, 0)
     gsend[0] = gram[:64]
     gsend[1] = gram[64:]
@@ -392,6 +434,7 @@
     squared = jnp.square(factor.astype(f32))
     nb[b, c] = dot(jnp.ones((8, RANK), f32), squared, 1, 1, precise)
 
+    sends_done()
     square = nb.at[b, c]
     n_z = [send(square, square, along_z(d)) for d in (2, 1, 7)]
     z_copies = []
@@ -412,38 +455,13 @@
     early_a = pass_on((a, b), (0, 1), up_a, down_a)
     basis = dot(raw_rows.astype(f32), lower, 1, 1, precise)[:OWN]
     p_all[c] = basis.astype(bf16)
-    p_copies = [send(p_all.at[c], p_all.at[c], {"island": lax.rem(c + d, 4)}) for d in (1, 2, 3)]
     p_own[...] = (basis * (error_decay - 1.0)).astype(bf16)
 
-    order = [lax.rem(m - c + 4, 4) for m in range(4)]
-
-    def finish(half, at, groups=((0, 1), (2, 3))):
-        for pieces in groups:
-            every = [
-                jnp.concatenate([f_all[half, i, at, order[m]] for m in range(4)], axis=0)
-                for i in pieces
-            ]
-            mean = dot(p_scaled[...], jnp.concatenate(every, axis=1), 1, 0)
-            own = [f_all[half, i, at, 0] for i in pieces]
-            decay = dot(p_own[...], jnp.concatenate(own, axis=1), 1, 0)
-            for n, i in enumerate(pieces):
-                lanes = slice(n * 128, n * 128 + 128)
-                columns = pl.ds(
-                    pl.multiple_of(half * (COLS // 2) + i * 512 + at * 128, 128), 128
-                )
-                matrix = grads_v[:, columns].astype(f32) + buffer_v[:, columns].astype(f32)
-                buffer_new[:, columns] = (matrix + decay[:, lanes]).astype(bf16)
-                means[...] = mean[:, lanes]
-                carried = jnp.concatenate(
-                    [mom_all[m, :, columns].astype(f32) for m in range(4)], axis=0
-                )
-                part = mean[:, lanes]
-                anchor_new[:, columns] = (
-                    anchor_v[:, columns].astype(f32)
-                    - outer_rate * (part + outer_beta * (outer_beta * carried + part))
-                ).astype(bf16)
-                rows = pl.ds(pl.multiple_of(c * QUARTER, 8), QUARTER)
-                momentum_new[:, columns] = outer_beta * mom_v[:, columns] + means[rows, :]
+    held = (f_all, p_scaled, p_own, mom_all, grads_v, buffer_v, anchor_v, mom_v)
+    outs = (anchor_new, buffer_new, momentum_new)
+
+    def finish(half, at):
+        finish_columns(c, half, at, held, outs, means)
 
     for copy in early_b:
         copy.wait_recv()
@@ -460,8 +478,7 @@
     for copy in z_copies:
         copy.wait_recv()
     up_copy, down_copy = pass_on((a, b), (1, 4), up_b, down_b)
-    line_receive(2)
-    line_send(4)
+    p_copies = [send(p_all.at[c], p_all.at[c], {"island": lax.rem(c + d, 4)}) for d in (1, 2, 3)]
     for copy in n_second:
         copy.wait_recv()
     na[a] = (nb[0] + nb[1]) + (nb[2] + nb[3])
@@ -473,6 +490,8 @@
     b_on += pass_on((a, b_above), (1, 2), down_b)
     below_up, below_down = pass_on((a, b_below), (1, 4), up_a, down_a)
     above_up, above_down = pass_on((a, b_above), (1, 4), up_a, down_a)
+    line_receive(2)
+    line_send(4)
     for copy in early_b_on + b_on:
         copy.wait_recv()
     far_up, far_down = pass_on((a, b_far), (0, 4), up_a, down_a)
@@ -532,17 +551,13 @@
     for copy in far_on:
         copy.wait_recv()
     far_cross[3].start()
-    for copy, at in zip(crossing[1:3], (a_below, a_above)):
-        copy.wait_recv()
-        finish(1 - k, at)
+    crossing[1].wait_recv()
+    finish(1 - k, a_below)
     finish(k, b_far)
-    for copy in far_cross[:3]:
-        copy.wait_recv()
-    finish(1 - k, a_far, ((b_below, b_above),))
-    far_cross[3].wait_recv()
-    finish(1 - k, a_far, ((b, b_far),))
-    started.extend(far_cross)
-    for copy in started:
+    for copy in crossing[2:] + far_cross:
+        copy.wait_recv()
+    sends_done()
+    for copy in far_cross:
         copy.wait_send()
 
 
@@ -557,23 +572,23 @@
             vmem((OWN, COLS), bf16),
             vmem((OWN, COLS), bf16),
             vmem((QUARTER, COLS), f32),
-        ),
-        in_specs=[anywhere] * 5,
-        out_specs=(whole, whole, whole),
-        scratch_shapes=[
             vmem((2, 4, 4, 4, *block), bf16),
             vmem((OWN, 4 * RANK), bf16),
             vmem((OWN, RANK), bf16),
             vmem((4, QUARTER, COLS), bf16),
             vmem((OWN, COLS), bf16),
+            vmem((OWN, COLS), bf16),
+            vmem((OWN, COLS), bf16),
+            vmem((QUARTER, COLS), f32),
+        ),
+        in_specs=[anywhere] * 5,
+        out_specs=(whole,) * 11,
+        scratch_shapes=[
             vmem((OWN, 128), f32),
             vmem((4, 4, 8, 128), f32),
             vmem((4, 4, 8, 128), f32),
             vmem((2, 4, 8, 128), f32),
             vmem((64, RANK), f32),
-            vmem((OWN, COLS), bf16),
-            vmem((OWN, COLS), bf16),
-            vmem((QUARTER, COLS), f32),
             vmem((PADDED, COLS), bf16),
             vmem((2, 2, PADDED, COLS // 4), bf16),
             vmem((2, 2, 4, 4, 64, RANK), bf16),
@@ -596,51 +611,75 @@
             vmem(block, bf16),
             vmem((4, OWN, RANK), bf16),
             pltpu.SemaphoreType.DMA((5,)),
-            pltpu.SemaphoreType.DMA((160,)),
-            pltpu.SemaphoreType.DMA((160,)),
+            pltpu.SemaphoreType.DMA((SENDS,)),
+            pltpu.SemaphoreType.DMA((RECEIVES,)),
         ],
         compiler_params=pltpu.CompilerParams(
-            collective_id=0, has_side_effects=True, vmem_limit_bytes=36 * 1024 * 1024
+            collective_id=0, has_side_effects=True, vmem_limit_bytes=32 * 1024 * 1024
         ),
         name="exchange",
     )(*(pltpu.with_memory_space_constraint(v, pltpu.HBM) for v in (grads, buffer, q_old, anchor, momentum)))
 
 
-def store_kernel(anchor_v, buffer_v, momentum_v, anchor_new, buffer_new, momentum_new, sems):
-    copies = []
-    for source, target, parts in (
-        (anchor_v, anchor_new, 7),
-        (buffer_v, buffer_new, 7),
-        (momentum_v, momentum_new, 7),
-    ):
-        height = source.shape[0] // parts
-        for part in range(parts):
-            rows = pl.ds(part * height, height)
-            copy = pltpu.make_async_copy(source.at[rows], target.at[rows], sems.at[len(copies)])
+def update_kernel(*refs):
+    done, held, outs, parts = refs[:3], refs[3:11], refs[11:14], refs[14:17]
+    means, *sems = refs[17:]
+    c = lax.axis_index("island")
+    x = lax.axis_index("fsdp_1")
+    y = lax.axis_index("fsdp_2")
+    k = lax.axis_index("fsdp_3")
+    a = x * (1 - k) + y * k
+
+    def copy_columns(sources, first, to, width):
+        for source, out, sem in zip(sources, outs, sems):
+            copy = pltpu.make_async_copy(
+                source.at[:, pl.ds(first, width)],
+                out.at[:, pl.ds(to, width)],
+                sem,
+            )
             copy.start()
-            copies.append(copy)
-    for copy in copies:
-        copy.wait()
-
-
-def store(anchor_new, buffer_new, momentum_new):
+
+    for quarter in range(2):
+        first = pl.multiple_of(k * (COLS // 2) + quarter * 1024, 1024)
+        copy_columns(done, first, first, 1024)
+    for at in (a, lax.rem(a + 3, 4)):
+        for i in range(4):
+            first = first_column(1 - k, i, at)
+            copy_columns(done, first, first, 128)
+    for n, at in enumerate((lax.rem(a + 1, 4), lax.rem(a + 2, 4))):
+        finish_columns(c, 1 - k, at, held, parts, means, place=n * 4)
+        for i in range(4):
+            copy_columns(parts, (n * 4 + i) * 128, first_column(1 - k, i, at), 128)
+    for source, out, sem in zip(done, outs, sems):
+        pltpu.make_async_copy(source, out, sem).wait()
+
+
+def update(*arrays):
     return pl.pallas_call(
-        store_kernel,
+        update_kernel,
         out_shape=(
             jax.ShapeDtypeStruct((OWN, COLS), bf16),
             jax.ShapeDtypeStruct((OWN, COLS), bf16),
             jax.ShapeDtypeStruct((QUARTER, COLS), f32),
         ),
-        in_specs=[pl.BlockSpec(memory_space=pltpu.VMEM)] * 3,
+        in_specs=[pl.BlockSpec(memory_space=pltpu.VMEM)] * 11,
         out_specs=[pl.BlockSpec(memory_space=pltpu.HBM)] * 3,
-        scratch_shapes=[pltpu.SemaphoreType.DMA((21,))],
-        compiler_params=pltpu.CompilerParams(vmem_limit_bytes=1024 * 1024),
-        name="store",
-    )(anchor_new, buffer_new, momentum_new)
+        scratch_shapes=[
+            pltpu.VMEM((OWN, 1024), bf16),
+            pltpu.VMEM((OWN, 1024), bf16),
+            pltpu.VMEM((QUARTER, 1024), f32),
+            pltpu.VMEM((OWN, 128), f32),
+            pltpu.SemaphoreType.DMA,
+            pltpu.SemaphoreType.DMA,
+            pltpu.SemaphoreType.DMA,
+        ],
+        compiler_params=pltpu.CompilerParams(vmem_limit_bytes=8 * 1024 * 1024),
+        name="update",
+    )(*arrays)
 
 
 def body(grads, buffer, q_old, anchor, momentum):
-    anchor_new, buffer_new, momentum_new = store(
+    anchor_new, buffer_new, momentum_new = update(
         *exchange(grads[0, 0], buffer[0], q_old[0], anchor, momentum)
     )
     return (anchor_new, buffer_new[None], momentum_new)

time: 71.2 us -> 69.5 us (0.976)
  Pallas kernels: 70.5 us -> 68.7 us
    pallas_call x1, Pallas kernels: 68.2 us -> 66.1 us  [exchange(): pl.pallas_call(exchange_kernel, out_shape=(vmem((OWN, COLS), bf16), vmem(...]
where the time goes in v5:
time: 69.5 us; the launch traced here: 69.4 us
  Pallas kernels  68.7 us (99%)
    pallas_call x1, Pallas kernels, exchange(): pl.pallas_call(exchange_kernel, out_shape=(vmem((OWN, COLS), bf16), vmem(...  66.1 us
    pallas_call x1, Pallas kernels, update(): pl.pallas_call(update_kernel, out_shape=(jax.ShapeDtypeStruct((OWN, COLS)...  2.63 us

profile of v5, /device:TPU:1, one launch (start us, length us, event | category | flops | bytes accessed | tf_op | source)
XLA Modules:
  0.0 69.4 jit_solution(1205506465498074498)
XLA Ops:
  0.6 66.1 %exchange.1 = (bf16[224,4096]{1,0:T(8,128)(2,1)S(1)}, bf16[224,4096]{1,0:T(8,128)(2,1)S(1)}, f32[56,4096]{1,0:T(8,128)S(1)}, bf16[2,4,4,4,128,128]{5,4,3,2,1,0:T...) custom-call(bf16[224,4096]{1,0:T(8,128)(2,1)} %bitcast.4, ...), custom_call_target="tpu_custom_call" | custom-call | tf_op jit(solution)/shard_map/exchange/pallas_call | solution.py:569
  66.8 2.6 %update.1 = (bf16[224,4096]{1,0:T(8,128)(2,1)}, bf16[224,4096]{1,0:T(8,128)(2,1)}, f32[56,4096]{1,0:T(8,128)}) custom-call(bf16[224,4096]{1,0:T(8,128)(2,1)S(1)} %get-tuple-element.17.refs_0_, bf16[224,4096]{1,0:T(8,128)(2,1)S(1)} %get-tuple-element.18.refs_1_, f32[56,4096]{1,0:T(8,128)S(1)} %get-tuple-element.19.refs_2_, ...), custom_call_target="tpu_custom_call" | custom-call | tf_op jit(solution)/shard_map/update/pallas_call | solution.py:658

commit v6 on v5

--- a/solution.py
+++ b/solution.py
@@ -16,7 +16,7 @@
 OWN = 224
 PADDED = 256
 QUARTER = 56
-SENDS, RECEIVES = 64, 115
+SENDS, RECEIVES = 64, 93
 MESH = pl.DeviceIdType.MESH
 
 precise = lax.Precision.HIGHEST
@@ -184,19 +184,19 @@
     free = list(range(SENDS))
     started = []
 
-    def copy_to(src, dst, device, at=None):
+    def copy_to(src, dst, device, at=None, arrival=None):
         return pltpu.make_async_remote_copy(
             src_ref=src,
             dst_ref=dst,
             send_sem=send_sem.at[free.pop() if at is None else at],
-            recv_sem=recv_sem.at[next(receives)],
+            recv_sem=recv_sem.at[next(receives) if arrival is None else arrival],
             device_id=device,
             device_id_type=MESH,
         )
 
-    def send(src, dst, device):
+    def send(src, dst, device, arrival=None):
         at = free.pop()
-        copy = copy_to(src, dst, device, at)
+        copy = copy_to(src, dst, device, at, arrival)
         copy.start()
         started.append((at, copy))
         return copy
@@ -224,8 +224,11 @@
     qa[h, k, a, b] = q_v[...].astype(bf16)
     pl.semaphore_wait(barrier, len(peers))
 
-    def along_second(part):
-        return [send(part, part, second_axis(d)) for d in (2, 1, 3)]
+    near_arrival, far_arrival = next(receives), next(receives)
+
+    def along_second(part, arrival):
+        for d in (2, 1, 3):
+            send(part, part, second_axis(d), arrival)
 
     def first_sends(part):
         return {d: send(part, part, first_axis(d)) for d in (2, 1, 3)}
@@ -234,10 +237,10 @@
     far_piece = qa.at[1 - h, k, a, b]
     q_far = send(own_piece, own_piece, other_half)
     q_first = first_sends(own_piece)
-    on_near = along_second(own_piece)
+    along_second(own_piece, near_arrival)
 
     line = []
-    for step, first, rows in ((1, 0, 56), (2, 0, 40), (2, 40, 16), (3, 0, 16), (3, 16, 40)):
+    for step, first, rows in ((1, 0, 56), (2, 0, 40), (2, 40, 16), (3, 0, 24), (3, 24, 32)):
         up_ok = jnp.logical_and(c < 3, c >= step - 1)
         down_ok = jnp.logical_and(c > 0, c + step - 1 <= 3)
         up_part = mom_all.at[lax.rem(c - (step - 1) + 4, 4), pl.ds(first, rows)]
@@ -313,23 +316,27 @@
         for core in (0, 1):
             mp[half, core, OWN:, :] = jnp.zeros((PADDED - OWN, COLS // 4), bf16)
 
-    def arrived(at, copies):
-        on = []
+    def arrived(at, copies, arrival):
         for d in (1, 3, 2):
             copies[d].wait_recv()
-            on += along_second(qa.at[at, k, lax.rem(a + 4 - d, 4), b])
-        return on
-
-    on_near += arrived(h, q_first)
+            along_second(qa.at[at, k, lax.rem(a + 4 - d, 4), b], arrival)
+
+    arrived(h, q_first, near_arrival)
     q_far.wait_recv()
     q_first = first_sends(far_piece)
-    on_far = along_second(far_piece)
-    on_far += arrived(1 - h, q_first)
-    q_second = [(h, on_near), (1 - h, on_far)]
+    along_second(far_piece, far_arrival)
+    arrived(1 - h, q_first, far_arrival)
     q_cross = []
-    for at, copies in q_second:
-        for copy in copies:
-            copy.wait_recv()
+    for at, arrival in ((h, near_arrival), (1 - h, far_arrival)):
+        twelve = qa.at[at, k, pl.ds(0, 3)]
+        pltpu.make_async_remote_copy(
+            src_ref=twelve,
+            dst_ref=twelve,
+            send_sem=send_sem.at[0],
+            recv_sem=recv_sem.at[arrival],
+            device_id=other_core,
+            device_id_type=MESH,
+        ).wait_recv()
         half = qa.at[at, k]
         q_cross.append((at, send(half, half, other_core)))
 

time: 69.5 us -> 69.7 us (level)
  no operation moved by 1% of the time
where the time goes in v6:
time: 69.7 us
  Pallas kernels  69 us (99%)
    pallas_call x1, Pallas kernels, exchange(): pl.pallas_call(exchange_kernel, out_shape=(vmem((OWN, COLS), bf16), vmem(...  66.4 us
    pallas_call x1, Pallas kernels, update(): pl.pallas_call(update_kernel, out_shape=(jax.ShapeDtypeStruct((OWN, COLS)...  2.63 us

profile of v6, /device:TPU:1, one launch (start us, length us, event | category | flops | bytes accessed | tf_op | source)
XLA Modules:
  0.0 69.7 jit_solution(1489346852293492482)
XLA Ops:
  0.6 66.4 %exchange.1 = (bf16[224,4096]{1,0:T(8,128)(2,1)S(1)}, bf16[224,4096]{1,0:T(8,128)(2,1)S(1)}, f32[56,4096]{1,0:T(8,128)S(1)}, bf16[2,4,4,4,128,128]{5,4,3,2,1,0:T...) custom-call(bf16[224,4096]{1,0:T(8,128)(2,1)} %bitcast.4, ...), custom_call_target="tpu_custom_call" | custom-call | tf_op jit(solution)/shard_map/exchange/pallas_call | solution.py:576
  67.0 2.6 %update.1 = (bf16[224,4096]{1,0:T(8,128)(2,1)}, bf16[224,4096]{1,0:T(8,128)(2,1)}, f32[56,4096]{1,0:T(8,128)}) custom-call(bf16[224,4096]{1,0:T(8,128)(2,1)S(1)} %get-tuple-element.17.refs_0_, bf16[224,4096]{1,0:T(8,128)(2,1)S(1)} %get-tuple-element.18.refs_1_, f32[56,4096]{1,0:T(8,128)S(1)} %get-tuple-element.19.refs_2_, ...), custom_call_target="tpu_custom_call" | custom-call | tf_op jit(solution)/shard_map/update/pallas_call | solution.py:665
